TPU v7x, 32 devices: a whole 2x2x4 slice. The times are simulated.
32 devices in a mesh: groups: 2 (over x), row: 16 (over z, y, core).
Axes of the slice: x: 2, y: 2, z: 4, core: 2. Of those that a mesh axis runs over, the one named last changes fastest.
Arguments:
- factor_b: bfloat16 [64, 131072], P(None, ('groups', 'row')), parts along dimension 1, may hold values from -12 to 12
- factor_c: bfloat16 [64, 131072], P(None, ('groups', 'row')), parts along dimension 1, may hold values from -12 to 12
- sample_j: int32 [262144], P(('groups', 'row')), parts along dimension 0, may hold values from 0 to 65535, as said below
- sample_k: int32 [16, 32, 512], P(None, ('groups', 'row')), parts along dimension 1, may hold values from 0 to 65535, as said below
- sample_weight: float32 [262144], P(('groups', 'row')), parts along dimension 0, may hold values from 0.5 to 3.5
- block_values: bfloat16 [32, 16, 4, 4, 128], P(('groups', 'row')), parts along dimension 0, may hold values from -24 to 24
- block_sample: int32 [32, 16, 4, 4], P(('groups', 'row')), parts along dimension 0, may hold values from 0 to 8191
- block_count: int32 [32, 16, 4, 4], P(('groups', 'row')), parts along dimension 0, may hold values from 0 to 128, as said below
Outputs:
- factor_new: bfloat16 [64, 16384], P(None, ('groups', 'row')), parts along dimension 1
- scales: float32 [128], P('groups'), parts along dimension 0
There are 2 independent parts, one for each index of `groups`. A program takes and returns all parts, laid end to end along the dimension named above; each array names one. Nothing has to cross between parts.
Inputs may be any that keep to these rules, and one draw needn't show every extreme that they name: sample_j[s] lies in rows s // 8192 * 4096 to s // 8192 * 4096 + 4095. sample_k[d, e, i] is the third-mode index of sample d * 8192 + e * 512 + i and lies in rows e * 4096 to e * 4096 + 4095. `block_count`: 0 marks an empty slot; slot [p, p, 0, 0] holds 128 for every p.
All inputs are finite; a program needn't handle non-finite values.
Results may differ from a plain program's by a relative error of at most 0.0051.
Values may be sent and summed in bfloat16 or wider, within the bound.
No kernel may reach another device: no remote copies, remote signals or barrier semaphores. Data moves between devices by JAX's collectives and lax.ppermute only.
A program may use at most 64 MiB of HBM per device.

v0:
```python
import jax
import jax.numpy as jnp
from jax import lax
from jax.sharding import PartitionSpec as P


def shards(
    factor_b, factor_c, sample_j, sample_k, sample_weight, block_values, block_sample, block_count
):
    rank_width = factor_b.shape[0]
    device_count = lax.axis_size("row")
    device_index = lax.axis_index("row")
    b_columns = jnp.take(factor_b, sample_j - device_index * factor_b.shape[1], axis=1)
    c_local = sample_k.reshape(-1) - device_index * factor_c.shape[1]
    c_outgoing = jnp.take(factor_c, c_local, axis=1).reshape(rank_width, device_count, -1)
    c_columns = lax.all_to_all(c_outgoing, "row", split_axis=1, concat_axis=1, tiled=True).reshape(
        rank_width, -1
    )
    sketch = sample_weight[None, :] * b_columns.astype(jnp.float32) * c_columns.astype(jnp.float32)
    gram_local = jnp.dot(sketch, sketch.T, precision=lax.Precision.HIGHEST)
    live_local = jnp.sum(block_count.astype(jnp.float32))
    gram_matrix, live_total = lax.psum((gram_local, live_local), "row")
    weighted = (sample_weight[None, :] * sketch).astype(jnp.bfloat16)
    positions = lax.broadcasted_iota(jnp.int32, block_values.shape, 4)
    masked = jnp.where(
        positions < block_count[..., None], block_values, jnp.zeros_like(block_values)
    )[0]
    tile_count = masked.shape[1]
    slot_count = masked.shape[2]
    weighted_rows = weighted.T
    picked = jnp.take(weighted_rows, block_sample.reshape(-1), axis=0)
    picked = picked.reshape(device_count, tile_count, slot_count, rank_width)
    values_in, rows_in = (
        lax.all_to_all(
            masked.reshape(device_count, -1), "row", split_axis=0, concat_axis=0, tiled=True
        ),
        lax.all_to_all(
            picked.reshape(device_count, -1), "row", split_axis=0, concat_axis=0, tiled=True
        ),
    )
    gathered = jnp.einsum(
        "stcr,stck->ktr",
        values_in.reshape(masked.shape),
        rows_in.reshape(picked.shape),
        preferred_element_type=jnp.float32,
    ).reshape(rank_width, -1)
    total_rows = gathered.shape[1] * device_count
    total_samples = sketch.shape[1] * device_count
    ridge = 0.05 * live_total / total_rows
    system = gram_matrix / total_samples + ridge * jnp.eye(rank_width, dtype=jnp.float32)
    lower_factor = jnp.linalg.cholesky(system)
    half_solved = lax.linalg.triangular_solve(lower_factor, gathered, left_side=True, lower=True)
    update = lax.linalg.triangular_solve(
        lower_factor, half_solved, left_side=True, lower=True, transpose_a=True
    )
    column_sums = lax.psum(jnp.sum(update * update, axis=1), "row")
    scales = jnp.sqrt(column_sums / total_rows + 1e-06)
    return ((update / scales[:, None]).astype(jnp.bfloat16), scales)


def solution(mesh):
    in_specs = (
        P(None, ("groups", "row")),
        P(None, ("groups", "row")),
        P(("groups", "row")),
        P(None, ("groups", "row"), None),
        P(("groups", "row")),
        P(("groups", "row"), None, None, None, None),
        P(("groups", "row"), None, None, None),
        P(("groups", "row"), None, None, None),
    )
    out_specs = (P(None, ("groups", "row")), P("groups"))
    return jax.shard_map(shards, mesh=mesh, in_specs=in_specs, out_specs=out_specs, check_vma=False)
```

profile of v0, /device:TPU:0, one launch (start us, length us, event | category | flops | bytes accessed | tf_op | source)
XLA Modules:
  0.0 222.7 jit_solution(864086933986388068)
XLA Ops:
  0.6 0.8 copy.44
  1.4 1.0 fusion.4
  2.4 0.5 broadcast.153
  3.0 1.0 reduce.8
  4.0 0.7 reshape.158
  4.6 7.4 %all-to-all-start.2 = ((bf16[16,2,1024]{2,1,0:T(2,128)(2,1)}), bf16[16,2,1024]{2,1,0:T(2,128)(2,1)S(1)}, u32[]{:S(2)}, u32[]{:S(2)}) async-start(bf16[16,2,1024]{2,1,0:T(2,128)(2,1)} %reshape.158), calls=%async_computation.2 | async-start | bytes 131072 | tf_op jit(solution)/shard_map/all_to_all | solution.py:34
  12.0 0.8 broadcast_subtract_fusion
  12.8 1.5 copy.37
  14.4 29.2 %gather_fusion.2 = bf16[8192,64]{1,0:T(8,128)(2,1)} fusion(bf16[64,4096]{0,1:T(8,128)(2,1)S(1)} %copy.37, s32[8192]{0:T(1024)S(1)} %fusion.12), kind=kCustom, calls=%fused_computation.1.clone | custom fusion | bytes 2129920 | tf_op jit(solution)/shard_map/jit(_take)/gather | solution.py:15
  43.6 5.8 %broadcast_select_fusion = bf16[8192,64]{1,0:T(8,128)(2,1)S(1)} fusion(bf16[8192,64]{1,0:T(8,128)(2,1)} %gather_fusion.2, pred[8192]{0:T(1024)(128)(4,1)S(1)} %compare_and_fusion), kind=kLoop, calls=%fused_computation.6 | loop fusion | flops 524288 | bytes 2105344 | tf_op jit(solution)/shard_map/jit(_take)/select_n | solution.py:15
  49.4 0.0 copy-start
  49.4 1.6 copy.38
  51.1 6.2 %all-to-all-start = ((bf16[64,16,512]{2,0,1:T(8,128)(2,1)}), bf16[64,16,512]{2,0,1:T(8,128)(2,1)}, u32[]{:S(2)}, u32[]{:S(2)}) async-start(bf16[64,16,512]{2,0,1:T(8,128)(2,1)} %copy.38), calls=%async_computation | async-start | bytes 2097152 | tf_op jit(solution)/shard_map/all_to_all | solution.py:16
  57.3 0.5 copy.36
  57.8 0.1 copy.42
  57.9 0.1 reshape.120
  58.0 0.1 copy.41
  58.1 0.1 broadcast_in_dim.30
  58.2 0.1 broadcast_in_dim.31
  58.4 0.0 copy-start.4
  58.4 24.0 %gather_fusion.1 = bf16[8192,64]{1,0:T(8,128)(2,1)S(1)} fusion(bf16[64,4096]{0,1:T(8,128)(2,1)S(1)} %copy.36, s32[8192]{0:T(1024)S(1)} %fusion.13), kind=kCustom, calls=%fused_computation.clone | custom fusion | bytes 2129920 | tf_op jit(solution)/shard_map/jit(_take)/gather | solution.py:13
  82.5 0.6 convert_reduce_fusion
  83.1 0.1 reshape.159
  83.1 0.4 reduce.7
  83.5 0.0 copy-start.2
  83.6 0.0 all-to-all-done
  83.6 3.3 %copy.39 = f32[64,16,512]{0,2,1:T(8,128)} copy(bf16[64,16,512]{2,0,1:T(8,128)(2,1)} %all-to-all-done) | data formatting | bytes 3145728 | tf_op jit(solution)/shard_map/convert_element_type | solution.py:19
  86.9 9.6 %fusion = (bf16[8192,64]{1,0:T(8,128)(2,1)}, f32[64,8192]{0,1:T(8,128)S(1)}) fusion(f32[8192]{0:T(1024)S(1)} %copy-done.2, f32[64,16,512]{0,2,1:T(8,128)} %copy.39, bf16[8192,64]{1,0:T(8,128)(2,1)S(1)} %gather_fusion.1, pred[8192]{0:T(1024)(128)(4,1)S(1)} %compare_and_fusion.1), kind=kLoop, calls=%fused_computation.5 | loop fusion | flops 3145728 | bytes 6332416 | tf_op jit(solution)/shard_map/transpose | solution.py:30
  96.5 7.0 %fusion.14 = f32[64,64]{1,0:T(8,128)S(1)} fusion(f32[64,8192]{0,1:T(8,128)S(1)} %get-tuple-element.6), kind=kOutput, calls=%fused_computation.43 | convolution fusion | flops 402653184 | bytes 2113536 | tf_op jit(solution)/shard_map/dot_general | solution.py:20
  103.5 63.0 %all-reduce = (f32[64,64]{1,0:T(8,128)S(1)}, f32[]{:T(128)}) all-reduce(f32[64,64]{1,0:T(8,128)S(1)} %fusion.14, f32[]{:T(128)} %convert_reduce_fusion), channel_id=1, replica_groups=mesh['groups'=2,'row'=16] {'row'}, use_global_device_ids=true, to_apply=%region_0.0 | all-reduce | flops 4097 | bytes 32776 | tf_op jit(solution)/shard_map/psum | solution.py:22
  167.1 0.1 copy.40
  167.2 5.8 %cholesky.16 = f32[64,64]{1,0:T(8,128)S(1)} custom-call(f32[64,64]{1,0:T(8,128)S(1)} %fusion.11), custom_call_target="Cholesky" | custom-call | tf_op jit(solution)/shard_map/jit(cholesky)/cholesky | solution.py:51
  173.1 0.7 compare_reduce_fusion
  173.8 2.6 %gather_fusion = bf16[256,64]{1,0:T(8,128)(2,1)S(1)} fusion(bf16[8192,64]{1,0:T(8,128)(2,1)} %get-tuple-element.5, s32[1024]{0:T(1024)S(1)} %pad_clamp_fusion), kind=kCustom, calls=%fused_computation.2 | custom fusion | bytes 66560 | tf_op jit(solution)/shard_map/jit(_take)/gather | solution.py:31
  176.4 0.1 gather.10
  176.6 0.7 reduce.9
  177.2 0.6 reshape.160
  177.8 3.5 %all-to-all-start.1 = ((bf16[16,2,512]{2,1,0:T(2,128)(2,1)}), bf16[16,2,512]{2,1,0:T(2,128)(2,1)S(1)}, u32[]{:S(2)}, u32[]{:S(2)}) async-start(bf16[16,2,512]{2,1,0:T(2,128)(2,1)} %reshape.160), calls=%async_computation.1 | async-start | bytes 65536 | tf_op jit(solution)/shard_map/all_to_all | solution.py:37
  181.4 0.7 fusion.7
  182.1 4.9 %custom-call.8 = f32[1,64,64]{1,2,0:T(8,128)S(1)} custom-call(f32[1,64,64]{2,1,0:T(8,128)S(1)} %fusion.7), custom_call_target="InvertDiagBlocksLowerTriangular" | custom-call | tf_op jit(solution)/shard_map/triangular_solve | solution.py:53
  187.0 1.0 all-to-all-done.1
  188.0 0.2 reduce.6
  188.2 0.1 reshape.121
  188.3 0.2 convolution_bitcast_fusion
  188.5 0.3 fusion.1
  188.8 0.4 multiply_reduce_fusion
  189.2 32.8 %psum.23 = f32[64]{0:T(128)S(1)} all-reduce(f32[64]{0:T(128)S(1)} %get-tuple-element.7), channel_id=1, replica_groups=mesh['groups'=2,'row'=16] {'row'}, use_global_device_ids=true, to_apply=%region_6.8 | all-reduce | flops 64 | bytes 512 | tf_op jit(solution)/shard_map/psum | solution.py:56
  222.0 0.7 divide_convert_fusion
  (25 shorter events, 0.3 us)
Async XLA Ops:
  4.6 46.5 %all-to-all-start.2 = ((bf16[16,2,1024]{2,1,0:T(2,128)(2,1)}), bf16[16,2,1024]{2,1,0:T(2,128)(2,1)S(1)}, u32[]{:S(2)}, u32[]{:S(2)}) async-start(bf16[16,2,1024]{2,1,0:T(2,128)(2,1)} %reshape.158), calls=%async_computation.2 | async-start | bytes 131072 | tf_op jit(solution)/shard_map/all_to_all | solution.py:34
  49.4 7.9 %copy-start = (bf16[64,4096]{1,0:T(8,128)(2,1)S(1)}, bf16[64,4096]{1,0:T(8,128)(2,1)}, u32[]{:S(2)}) copy-start(bf16[64,4096]{1,0:T(8,128)(2,1)} %param.10) | copy-start | bytes 1572868
  51.1 6.7 %copy-start.3 = (s32[1,16,4,4]{1,3,2,0:T(4,128)S(1)}, s32[1,16,4,4]{1,3,2,0:T(4,128)}, u32[]{:S(2)}) copy-start(s32[1,16,4,4]{1,3,2,0:T(4,128)} %param.16) | copy-start | bytes 3076
  51.1 7.3 %copy-start.1 = (s32[8192]{0:T(1024)S(1)}, s32[8192]{0:T(1024)}, u32[]{:S(2)}) copy-start(s32[8192]{0:T(1024)} %param.12) | copy-start | bytes 98308
  51.1 32.5 %all-to-all-start = ((bf16[64,16,512]{2,0,1:T(8,128)(2,1)}), bf16[64,16,512]{2,0,1:T(8,128)(2,1)}, u32[]{:S(2)}, u32[]{:S(2)}) async-start(bf16[64,16,512]{2,0,1:T(8,128)(2,1)} %copy.38), calls=%async_computation | async-start | bytes 2097152 | tf_op jit(solution)/shard_map/all_to_all | solution.py:16
  58.4 24.1 %copy-start.4 = (s32[1,16,4,4]{1,3,2,0:T(4,128)S(1)}, s32[1,16,4,4]{1,3,2,0:T(4,128)}, u32[]{:S(2)}) copy-start(s32[1,16,4,4]{1,3,2,0:T(4,128)} %param.17) | copy-start | bytes 3076
  83.5 3.3 %copy-start.2 = (f32[8192]{0:T(1024)S(1)}, f32[8192]{0:T(1024)}, u32[]{:S(2)}) copy-start(f32[8192]{0:T(1024)} %param.14) | copy-start | bytes 98308
  177.8 10.1 %all-to-all-start.1 = ((bf16[16,2,512]{2,1,0:T(2,128)(2,1)}), bf16[16,2,512]{2,1,0:T(2,128)(2,1)S(1)}, u32[]{:S(2)}, u32[]{:S(2)}) async-start(bf16[16,2,512]{2,1,0:T(2,128)(2,1)} %reshape.160), calls=%async_computation.1 | async-start | bytes 65536 | tf_op jit(solution)/shard_map/all_to_all | solution.py:37
  222.0 0.7 copy-start.5
where the time goes:
time: 224 us; the launch traced here: 223 us
  blocking collectives  95.8 us (43%)
  local copies, waits for them, and re-layouts  66.4 us (30%)
  other arithmetic  33 us (15%)
  starting transfers between devices  17.1 us (8%)
  matrix products  7.89 us (4%)
    psum x1, blocking collectives, shards(): gram_matrix, live_total = lax.psum((gram_local, live_local), 'row')  63 us
    psum x1, blocking collectives, shards(): column_sums = lax.psum(jnp.sum(update * update, axis=1), 'row')  32.8 us
    gather x1, local copies, waits for them, and re-layouts, shards(): jnp.take(factor_c, c_local, axis=1).reshape(rank_width, device_count, -1)  29.2 us
    gather x1, local copies, waits for them, and re-layouts, shards(): jnp.take(factor_b, sample_j - device_index * factor_b.shape[1], axis=1)  24 us
    transpose x1, other arithmetic, shards(): weighted_rows = weighted.T  9.6 us
    all_to_all x1, starting transfers between devices, shards(): lax.all_to_all(masked.reshape(device_count, -1), 'row', split_axis=0, con...  7.41 us
    dot_general x1, matrix products, shards(): gram_local = jnp.dot(sketch, sketch.T, precision=lax.Precision.HIGHEST)  7 us
    another operation x3, other arithmetic, shards(): lower_factor = jnp.linalg.cholesky(system)  6.6 us
  transfers between devices with their start and end apart: 3, of which 1 were waited for; matrix products, arithmetic and copies ran while one was open for 32% of the time, Pallas kernels for 0%

commit v1 on v0

--- a/solution.py
+++ b/solution.py
@@ -19,7 +19,11 @@
     sketch = sample_weight[None, :] * b_columns.astype(jnp.float32) * c_columns.astype(jnp.float32)
     gram_local = jnp.dot(sketch, sketch.T, precision=lax.Precision.HIGHEST)
     live_local = jnp.sum(block_count.astype(jnp.float32))
-    gram_matrix, live_total = lax.psum((gram_local, live_local), "row")
+    live_row = jnp.full((1, rank_width), live_local, jnp.float32)
+    pieces = lax.all_gather(jnp.concatenate([gram_local, live_row], axis=0), "row")
+    summed = jnp.sum(pieces, axis=0)
+    gram_matrix = summed[:rank_width]
+    live_total = summed[rank_width, 0]
     weighted = (sample_weight[None, :] * sketch).astype(jnp.bfloat16)
     positions = lax.broadcasted_iota(jnp.int32, block_values.shape, 4)
     masked = jnp.where(
@@ -53,7 +57,7 @@
     update = lax.linalg.triangular_solve(
         lower_factor, half_solved, left_side=True, lower=True, transpose_a=True
     )
-    column_sums = lax.psum(jnp.sum(update * update, axis=1), "row")
+    column_sums = jnp.sum(lax.all_gather(jnp.sum(update * update, axis=1), "row"), axis=0)
     scales = jnp.sqrt(column_sums / total_rows + 1e-06)
     return ((update / scales[:, None]).astype(jnp.bfloat16), scales)
 

time: 224 us -> 187 us (0.83)
  blocking collectives: 95.8 us -> 56.2 us
    psum x2 -> x0, blocking collectives: 95.8 us -> none  [the longest x1 63 us: shards(): gram_matrix, live_total = lax.psum((gram_local, live_local), 'row')]
    unnamed x0 -> x1, blocking collectives: none -> 32.8 us
    all_gather x0 -> x1, blocking collectives: none -> 23.4 us  [shards(): lax.all_gather(jnp.concatenate([gram_local, live_row], axis=0), 'row')]
    unnamed x19 -> x26, local copies, waits for them, and re-layouts: 3.51 us -> 5.08 us
  transfers between devices with their start and end apart: 3 -> 3, of which waited for: 1 -> 1; matrix products, arithmetic and copies ran while one was open for 32% -> 38% of each run, Pallas kernels for 0% -> 0%
where the time goes in v1:
time: 187 us; the launch traced here: 186 us
  local copies, waits for them, and re-layouts  68.6 us (37%)
  blocking collectives  56.2 us (30%)
  other arithmetic  33 us (18%)
  starting transfers between devices  17.1 us (9%)
  matrix products  7.88 us (4%)
  between operations  2.29 us (1%)
    unnamed x1, blocking collectives  32.8 us
    gather x1, local copies, waits for them, and re-layouts, shards(): jnp.take(factor_c, c_local, axis=1).reshape(rank_width, device_count, -1)  29.2 us
    gather x1, local copies, waits for them, and re-layouts, shards(): jnp.take(factor_b, sample_j - device_index * factor_b.shape[1], axis=1)  24 us
    all_gather x1, blocking collectives, shards(): lax.all_gather(jnp.concatenate([gram_local, live_row], axis=0), 'row')  23.4 us
    transpose x1, other arithmetic, shards(): weighted_rows = weighted.T  9.6 us
    all_to_all x1, starting transfers between devices, shards(): lax.all_to_all(masked.reshape(device_count, -1), 'row', split_axis=0, con...  7.41 us
    dot_general x1, matrix products, shards(): gram_local = jnp.dot(sketch, sketch.T, precision=lax.Precision.HIGHEST)  6.98 us
    another operation x3, other arithmetic, shards(): lower_factor = jnp.linalg.cholesky(system)  6.6 us
  transfers between devices with their start and end apart: 3, of which 1 were waited for; matrix products, arithmetic and copies ran while one was open for 38% of the time, Pallas kernels for 0%

profile of v1, /device:TPU:0, one launch (start us, length us, event | category | flops | bytes accessed | tf_op | source)
XLA Modules:
  0.0 186.1 jit_solution(15060287919482922318)
XLA Ops:
  0.6 0.8 copy.60
  1.4 1.0 fusion.4
  2.4 0.5 broadcast.163
  3.0 1.0 reduce.9
  4.0 0.7 reshape.174
  4.6 7.4 %all-to-all-start.2 = ((bf16[16,2,1024]{2,1,0:T(2,128)(2,1)}), bf16[16,2,1024]{2,1,0:T(2,128)(2,1)S(1)}, u32[]{:S(2)}, u32[]{:S(2)}) async-start(bf16[16,2,1024]{2,1,0:T(2,128)(2,1)} %reshape.174), calls=%async_computation.2 | async-start | bytes 131072 | tf_op jit(solution)/shard_map/all_to_all | solution.py:38
  12.0 0.8 broadcast_subtract_fusion
  12.8 1.5 copy.52
  14.4 29.2 %gather_fusion.2 = bf16[8192,64]{1,0:T(8,128)(2,1)} fusion(bf16[64,4096]{0,1:T(8,128)(2,1)S(1)} %copy.52, s32[8192]{0:T(1024)S(1)} %fusion.12), kind=kCustom, calls=%fused_computation.1.clone | custom fusion | bytes 2129920 | tf_op jit(solution)/shard_map/jit(_take)/gather | solution.py:15
  43.6 5.8 %broadcast_select_fusion = bf16[8192,64]{1,0:T(8,128)(2,1)S(1)} fusion(bf16[8192,64]{1,0:T(8,128)(2,1)} %gather_fusion.2, pred[8192]{0:T(1024)(128)(4,1)S(1)} %compare_and_fusion), kind=kLoop, calls=%fused_computation.6 | loop fusion | flops 524288 | bytes 2105344 | tf_op jit(solution)/shard_map/jit(_take)/select_n | solution.py:15
  49.4 1.6 copy.53
  51.1 6.2 %all-to-all-start = ((bf16[64,16,512]{2,0,1:T(8,128)(2,1)}), bf16[64,16,512]{2,0,1:T(8,128)(2,1)}, u32[]{:S(2)}, u32[]{:S(2)}) async-start(bf16[64,16,512]{2,0,1:T(8,128)(2,1)} %copy.53), calls=%async_computation | async-start | bytes 2097152 | tf_op jit(solution)/shard_map/all_to_all | solution.py:16
  57.3 0.5 copy.51
  57.8 0.1 copy.58
  57.9 0.1 reshape.126
  58.0 0.1 copy.57
  58.1 0.1 broadcast_in_dim.31
  58.2 0.1 broadcast_in_dim.32
  58.4 24.0 %gather_fusion.1 = bf16[8192,64]{1,0:T(8,128)(2,1)S(1)} fusion(bf16[64,4096]{0,1:T(8,128)(2,1)S(1)} %copy.51, s32[8192]{0:T(1024)S(1)} %fusion.13), kind=kCustom, calls=%fused_computation.clone | custom fusion | bytes 2129920 | tf_op jit(solution)/shard_map/jit(_take)/gather | solution.py:13
  82.5 0.6 dynamic-slice
  83.7 0.6 convert_reduce_fusion
  84.4 0.4 reduce.8
  84.8 3.3 %copy.54 = f32[64,16,512]{0,2,1:T(8,128)} copy(bf16[64,16,512]{2,0,1:T(8,128)(2,1)} %all-to-all-done) | data formatting | bytes 3145728 | tf_op jit(solution)/shard_map/convert_element_type | solution.py:19
  88.2 9.6 %fusion = (bf16[8192,64]{1,0:T(8,128)(2,1)}, f32[64,8192]{0,1:T(8,128)S(1)}) fusion(f32[8192]{0:T(1024)S(1)} %copy-done.2, f32[64,16,512]{0,2,1:T(8,128)} %copy.54, bf16[8192,64]{1,0:T(8,128)(2,1)S(1)} %gather_fusion.1, pred[8192]{0:T(1024)(128)(4,1)S(1)} %compare_and_fusion.1), kind=kLoop, calls=%fused_computation.5 | loop fusion | flops 3145728 | bytes 6332416 | tf_op jit(solution)/shard_map/transpose | solution.py:34
  97.8 7.0 %fusion.14 = f32[64,64]{0,1:T(8,128)S(1)} fusion(f32[64,8192]{0,1:T(8,128)S(1)} %get-tuple-element.4), kind=kOutput, calls=%fused_computation.44 | convolution fusion | flops 402653184 | bytes 2113536 | tf_op jit(solution)/shard_map/dot_general | solution.py:20
  104.7 0.7 pad_bitcast_fusion
  105.4 23.4 %all-gather.2 = f32[16,65,64]{1,2,0:T(8,128)S(1)} all-gather(f32[1,65,64]{1,2,0:T(8,128)S(1)} %pad_bitcast_fusion), channel_id=2, replica_groups=mesh['groups'=2,'row'=16] {'row'}, dimensions={0}, use_global_device_ids=true | all-gather | bytes 282880 | tf_op jit(solution)/shard_map/all_gather | solution.py:23
  128.8 0.6 slice.29
  129.4 0.1 copy.66
  130.2 0.1 copy.56
  130.3 5.8 %cholesky.16 = f32[64,64]{1,0:T(8,128)S(1)} custom-call(f32[64,64]{1,0:T(8,128)S(1)} %fusion.11), custom_call_target="Cholesky" | custom-call | tf_op jit(solution)/shard_map/jit(cholesky)/cholesky | solution.py:55
  136.2 0.7 compare_reduce_fusion
  136.9 2.6 %gather_fusion = bf16[256,64]{1,0:T(8,128)(2,1)S(1)} fusion(bf16[8192,64]{1,0:T(8,128)(2,1)} %get-tuple-element.3, s32[1024]{0:T(1024)S(1)} %pad_clamp_fusion), kind=kCustom, calls=%fused_computation.2 | custom fusion | bytes 66560 | tf_op jit(solution)/shard_map/jit(_take)/gather | solution.py:35
  139.5 0.1 gather.10
  139.6 0.7 reduce.10
  140.3 0.6 reshape.176
  140.9 3.5 %all-to-all-start.1 = ((bf16[16,2,512]{2,1,0:T(2,128)(2,1)}), bf16[16,2,512]{2,1,0:T(2,128)(2,1)S(1)}, u32[]{:S(2)}, u32[]{:S(2)}) async-start(bf16[16,2,512]{2,1,0:T(2,128)(2,1)} %reshape.176), calls=%async_computation.1 | async-start | bytes 65536 | tf_op jit(solution)/shard_map/all_to_all | solution.py:41
  144.4 0.7 fusion.7
  145.1 4.9 %custom-call.8 = f32[1,64,64]{1,2,0:T(8,128)S(1)} custom-call(f32[1,64,64]{2,1,0:T(8,128)S(1)} %fusion.7), custom_call_target="InvertDiagBlocksLowerTriangular" | custom-call | tf_op jit(solution)/shard_map/triangular_solve | solution.py:57
  150.0 1.0 all-to-all-done.1
  151.0 0.2 reduce.7
  151.2 0.1 reshape.127
  151.3 0.2 convolution_bitcast_fusion
  151.5 0.3 fusion.1
  151.9 0.4 multiply_reduce_fusion
  152.2 0.2 dynamic-update-slice.3
  152.5 32.8 %all-reduce.1 = f32[1024]{0:T(1024)S(1)} all-reduce(f32[1024]{0:T(1024)S(1)} %dynamic-update-slice.3), channel_id=3, replica_groups=mesh['groups'=2,'row'=16] {'row'}, use_global_device_ids=true, to_apply=%add.1 | all-reduce | flops 1024 | bytes 8192
  185.4 0.7 divide_convert_fusion
  (36 shorter events, 0.5 us)
Async XLA Ops:
  4.6 46.5 %all-to-all-start.2 = ((bf16[16,2,1024]{2,1,0:T(2,128)(2,1)}), bf16[16,2,1024]{2,1,0:T(2,128)(2,1)S(1)}, u32[]{:S(2)}, u32[]{:S(2)}) async-start(bf16[16,2,1024]{2,1,0:T(2,128)(2,1)} %reshape.174), calls=%async_computation.2 | async-start | bytes 131072 | tf_op jit(solution)/shard_map/all_to_all | solution.py:38
  49.4 7.9 %copy-start = (bf16[64,4096]{1,0:T(8,128)(2,1)S(1)}, bf16[64,4096]{1,0:T(8,128)(2,1)}, u32[]{:S(2)}) copy-start(bf16[64,4096]{1,0:T(8,128)(2,1)} %param.10) | copy-start | bytes 1572868
  51.1 6.7 %copy-start.3 = (s32[1,16,4,4]{1,3,2,0:T(4,128)S(1)}, s32[1,16,4,4]{1,3,2,0:T(4,128)}, u32[]{:S(2)}) copy-start(s32[1,16,4,4]{1,3,2,0:T(4,128)} %param.16) | copy-start | bytes 3076
  51.1 7.3 %copy-start.1 = (s32[8192]{0:T(1024)S(1)}, s32[8192]{0:T(1024)}, u32[]{:S(2)}) copy-start(s32[8192]{0:T(1024)} %param.12) | copy-start | bytes 98308
  51.1 33.7 %all-to-all-start = ((bf16[64,16,512]{2,0,1:T(8,128)(2,1)}), bf16[64,16,512]{2,0,1:T(8,128)(2,1)}, u32[]{:S(2)}, u32[]{:S(2)}) async-start(bf16[64,16,512]{2,0,1:T(8,128)(2,1)} %copy.53), calls=%async_computation | async-start | bytes 2097152 | tf_op jit(solution)/shard_map/all_to_all | solution.py:16
  58.4 24.1 %copy-start.6 = (u32[32]{0:T(128)S(1)}, u32[32]{0:T(128)}, u32[]{:S(2)}) copy-start(u32[32]{0:T(128)} %constant.103) | copy-start | bytes 388
  58.4 25.3 %copy-start.4 = (s32[1,16,4,4]{1,3,2,0:T(4,128)S(1)}, s32[1,16,4,4]{1,3,2,0:T(4,128)}, u32[]{:S(2)}) copy-start(s32[1,16,4,4]{1,3,2,0:T(4,128)} %param.17) | copy-start | bytes 3076
  84.8 3.3 %copy-start.2 = (f32[8192]{0:T(1024)S(1)}, f32[8192]{0:T(1024)}, u32[]{:S(2)}) copy-start(f32[8192]{0:T(1024)} %param.14) | copy-start | bytes 98308
  140.9 10.1 %all-to-all-start.1 = ((bf16[16,2,512]{2,1,0:T(2,128)(2,1)}), bf16[16,2,512]{2,1,0:T(2,128)(2,1)S(1)}, u32[]{:S(2)}, u32[]{:S(2)}) async-start(bf16[16,2,512]{2,1,0:T(2,128)(2,1)} %reshape.176), calls=%async_computation.1 | async-start | bytes 65536 | tf_op jit(solution)/shard_map/all_to_all | solution.py:41
  185.4 0.7 copy-start.5

commit v2 on v0

v2 whole, which is shorter than its diff:
```python
import functools

import jax
import jax.numpy as jnp
from jax import lax
from jax.experimental import pallas as pl
from jax.experimental.pallas import tpu as pltpu
from jax.sharding import PartitionSpec as P

LANES = 128
HIGHEST = lax.Precision.HIGHEST
VMEM = pl.BlockSpec(memory_space=pltpu.VMEM)
SMEM = pl.BlockSpec(memory_space=pltpu.SMEM)
OVER_ROWS = (((0,), (0,)), ((), ()))


def lane_index(shape):
    return lax.broadcasted_iota(jnp.int32, shape, 1)


def fill_table(factor_ref, table_ref):
    columns = factor_ref.shape[1]

    def step(chunk, carry):
        start = pl.multiple_of(chunk * LANES, LANES)
        block = factor_ref[:, pl.ds(start, LANES)].astype(jnp.float32)
        table_ref[pl.ds(start, LANES), :] = jnp.concatenate([block, block], axis=0).T
        return carry

    lax.fori_loop(0, columns // LANES, step, 0)


def gather_pairs(base_ref, index_ref, table_ref, rows_ref, span):
    half = span // 2
    step_rows = min(32, half)
    low = lane_index((1, LANES)) < LANES // 2
    base = base_ref[0]

    def step(q, carry):
        row = q * step_rows
        first = row + lax.div(row, half) * half
        for u in range(step_rows):
            a = index_ref[first + u] - base
            b = index_ref[first + (u + half)] - base
            rows_ref[pl.ds(row + u, 1), :] = jnp.where(
                low, table_ref[pl.ds(a, 1), :], table_ref[pl.ds(b, 1), :]
            )
        return carry

    lax.fori_loop(0, rows_ref.shape[0] // step_rows, step, 0)


def outgoing_kernel(base_ref, index_ref, factor_ref, out_ref, table_ref, rows_ref, *, span):
    fill_table(factor_ref, table_ref)
    gather_pairs(base_ref, index_ref, table_ref, rows_ref, span)
    out_ref[...] = rows_ref[...].astype(jnp.bfloat16)


def weighted_b_kernel(base_ref, index_ref, weight_ref, factor_ref, out_ref, table_ref, *, span):
    half = span // 2
    fill_table(factor_ref, table_ref)
    gather_pairs(base_ref, index_ref, table_ref, out_ref, span)
    turned = weight_ref[...].T
    low = lane_index((half, LANES)) < LANES // 2
    for e in range(out_ref.shape[0] // half):
        weights = jnp.where(low, turned[:, 2 * e : 2 * e + 1], turned[:, 2 * e + 1 : 2 * e + 2])
        out_ref[e * half : (e + 1) * half, :] = out_ref[e * half : (e + 1) * half, :] * weights


def sketch_kernel(
    sample_ref, count_ref, weight_ref, wb_ref, c_ref, values_ref, out_ref, sketch_ref, values32_ref, *, span
):
    half = span // 2
    total_rows = wb_ref.shape[0]
    devices, _, _ = out_ref.shape
    blocks = values_ref.shape[0] // devices
    chunk = min(512, total_rows)

    def gram_step(q, acc):
        start = pl.multiple_of(q * chunk, chunk)
        x = wb_ref[pl.ds(start, chunk), :] * c_ref[pl.ds(start, chunk), :].astype(jnp.float32)
        sketch_ref[pl.ds(start, chunk), :] = x
        high = x.astype(jnp.bfloat16)
        rest = (x - high.astype(jnp.float32)).astype(jnp.bfloat16)
        both = jnp.concatenate([high, rest], axis=1)
        return acc + lax.dot_general(high, both, OVER_ROWS, preferred_element_type=jnp.float32)

    acc = lax.fori_loop(
        0, total_rows // chunk, gram_step, jnp.zeros((LANES, 2 * LANES), jnp.float32)
    )
    rank = LANES // 2
    cross = acc[:, LANES:]
    full = acc[:, :LANES] + cross + cross.T
    gram = full[:rank] + pltpu.roll(full[rank:], rank, 1)
    low = lane_index((1, LANES)) < rank
    packed = jnp.where(low, gram[: rank // 2], pltpu.roll(gram[rank // 2 :], rank, 1))
    lane = lane_index((1, LANES))
    values32_ref[...] = values_ref[...].astype(jnp.float32)

    def count_step(q, total):
        for u in range(blocks):
            total = total + count_ref[q * blocks + u]
        return total

    live = lax.fori_loop(0, devices, count_step, jnp.int32(0)).astype(jnp.float32)

    def pick_step(q, carry):
        for u in range(blocks):
            j = q * blocks + u
            s = sample_ref[j]
            e = lax.div(s, span)
            i = s - e * span
            upper = i >= half
            row = e * half + jnp.where(upper, i - half, i)
            scaled = sketch_ref[pl.ds(row, 1), :] * weight_ref[s]
            picked = jnp.where(upper, pltpu.roll(scaled, rank, 1), scaled)
            rounded = picked.astype(jnp.bfloat16).astype(jnp.float32)
            out_ref[q, blocks + u : blocks + u + 1, :] = jnp.where(low, rounded, live)
            value_row = values32_ref[pl.ds(j, 1), :]
            out_ref[q, u : u + 1, :] = jnp.where(lane < count_ref[j], value_row, 0.0)
        out_ref[q, 2 * blocks :, :] = packed
        return carry

    lax.fori_loop(0, devices, pick_step, 0)


def solve_kernel(in_ref, update_ref, sums_ref, *, tiles, slots, total_rows, total_samples):
    devices = in_ref.shape[0]
    rank = LANES // 2
    blocks = tiles * slots
    summed = in_ref[0, 2 * blocks :, :]
    live_row = in_ref[0, blocks : blocks + 1, :]
    for p in range(1, devices):
        summed = summed + in_ref[p, 2 * blocks :, :]
        live_row = live_row + in_ref[p, blocks : blocks + 1, :]
    gram = jnp.concatenate([summed, pltpu.roll(summed, rank, 1)], axis=0)
    ridge = 0.05 * pltpu.roll(live_row, rank, 1)[:, 0:1] / total_rows
    lane = lane_index((rank, LANES))
    sub = lax.broadcasted_iota(jnp.int32, (rank, LANES), 0)
    state = gram / total_samples + jnp.where(lane == sub, ridge, 0.0)
    lane_row = lane_index((1, LANES))
    for k in range(rank):
        pivot = 1.0 / state[k : k + 1, k : k + 1]
        row = jnp.where(lane_row == k, 1.0, state[k : k + 1, :]) * pivot
        column = state[:, k : k + 1]
        rest = jnp.where(lane == k, 0.0, state)
        state = jnp.where(sub == k, row, rest - column * row)
    inverse = state[:, :rank]
    values = in_ref[:, :blocks, :].reshape(devices * blocks, LANES).astype(jnp.bfloat16)
    rows = in_ref[:, blocks : 2 * blocks, :].reshape(devices * blocks, LANES)
    wide = lane_index(rows.shape)
    doubled = jnp.where(wide < rank, rows, pltpu.roll(rows, rank, 1))
    tile_of = lax.div(
        lax.rem(lax.broadcasted_iota(jnp.int32, rows.shape, 0), blocks), slots
    )
    parts = []
    for g in range(0, tiles, 2):
        wanted = jnp.where(wide < rank, g, g + 1)
        left = jnp.where(tile_of == wanted, doubled, 0.0).astype(jnp.bfloat16)
        both = lax.dot_general(left, values, OVER_ROWS, preferred_element_type=jnp.float32)
        parts += [both[:rank], both[rank:]]
    gathered = jnp.concatenate(parts[:tiles], axis=1)
    update = jnp.dot(inverse, gathered, precision=HIGHEST, preferred_element_type=jnp.float32)
    update_ref[...] = update
    column_sums = jnp.sum(update * update, axis=1, keepdims=True)
    turned = jnp.broadcast_to(
        jnp.concatenate([column_sums, column_sums], axis=0), (LANES, LANES)
    ).T
    for p in range(devices):
        sums_ref[p] = turned[:8]


def scale_kernel(sums_ref, update_ref, out_ref, scales_ref, *, total_rows):
    rank = update_ref.shape[0]
    summed = sums_ref[0]
    for p in range(1, sums_ref.shape[0]):
        summed = summed + sums_ref[p]
    scales = jnp.sqrt(summed / total_rows + 1e-06)
    scales_ref[...] = scales
    column = jnp.broadcast_to(scales[0:1], (LANES, LANES)).T[:rank, 0:1]
    out_ref[...] = (update_ref[...] / column).astype(jnp.bfloat16)


def shape(dims, dtype):
    return jax.ShapeDtypeStruct(dims, dtype)


def shards(
    factor_b, factor_c, sample_j, sample_k, sample_weight, block_values, block_sample, block_count
):
    rank = factor_b.shape[0]
    devices = lax.axis_size("row")
    position = lax.axis_index("row")
    span = sample_k.shape[2]
    samples = sample_j.shape[0]
    tiles, slots, lanes = block_values.shape[2:]
    assert 2 * rank == LANES and lanes == LANES
    pairs = samples // 2
    f32 = jnp.float32
    c_base = jnp.full((1,), position * factor_c.shape[1], jnp.int32)
    b_base = jnp.full((1,), position * factor_b.shape[1], jnp.int32)
    c_out = pl.pallas_call(
        functools.partial(outgoing_kernel, span=span),
        out_shape=shape((pairs, LANES), jnp.bfloat16),
        in_specs=[SMEM, SMEM, VMEM],
        out_specs=VMEM,
        scratch_shapes=[
            pltpu.VMEM((factor_c.shape[1], LANES), f32),
            pltpu.VMEM((pairs, LANES), f32),
        ],
        name="outgoing",
    )(c_base, sample_k.reshape(-1), factor_c)
    c_in = lax.all_to_all(
        c_out.reshape(devices, pairs // devices, LANES), "row", split_axis=0, concat_axis=0, tiled=True
    ).reshape(pairs, LANES)
    weighted_b = pl.pallas_call(
        functools.partial(weighted_b_kernel, span=span),
        out_shape=shape((pairs, LANES), f32),
        in_specs=[SMEM, SMEM, VMEM, VMEM],
        out_specs=VMEM,
        scratch_shapes=[pltpu.VMEM((factor_b.shape[1], LANES), f32)],
        name="weighted_b",
    )(b_base, sample_j, sample_weight.reshape(2 * devices, span // 2), factor_b)
    blocks = tiles * slots
    payload = pl.pallas_call(
        functools.partial(sketch_kernel, span=span),
        out_shape=shape((devices, 2 * blocks + rank // 2, LANES), f32),
        in_specs=[SMEM, SMEM, SMEM, VMEM, VMEM, VMEM],
        out_specs=VMEM,
        scratch_shapes=[
            pltpu.VMEM((pairs, LANES), f32),
            pltpu.VMEM((devices * blocks, LANES), f32),
        ],
        name="sketch",
    )(
        block_sample.reshape(-1),
        block_count.reshape(-1),
        sample_weight,
        weighted_b,
        c_in,
        block_values.reshape(devices * blocks, LANES),
    )
    received = lax.all_to_all(payload, "row", split_axis=0, concat_axis=0, tiled=True)
    total_rows = tiles * LANES * devices
    update, sums = pl.pallas_call(
        functools.partial(
            solve_kernel,
            tiles=tiles,
            slots=slots,
            total_rows=total_rows,
            total_samples=samples * devices,
        ),
        out_shape=(shape((rank, tiles * LANES), f32), shape((devices, 8, LANES), f32)),
        in_specs=[VMEM],
        out_specs=(VMEM, VMEM),
        name="solve",
    )(received)
    all_sums = lax.all_to_all(sums, "row", split_axis=0, concat_axis=0, tiled=True)
    factor_new, scales = pl.pallas_call(
        functools.partial(scale_kernel, total_rows=total_rows),
        out_shape=(shape((rank, tiles * LANES), jnp.bfloat16), shape((8, LANES), f32)),
        in_specs=[VMEM, VMEM],
        out_specs=(VMEM, VMEM),
        name="scale",
    )(all_sums, update)
    return factor_new, scales[0, :rank]


def solution(mesh):
    in_specs = (
        P(None, ("groups", "row")),
        P(None, ("groups", "row")),
        P(("groups", "row")),
        P(None, ("groups", "row"), None),
        P(("groups", "row")),
        P(("groups", "row"), None, None, None, None),
        P(("groups", "row"), None, None, None),
        P(("groups", "row"), None, None, None),
    )
    out_specs = (P(None, ("groups", "row")), P("groups"))
    return jax.shard_map(shards, mesh=mesh, in_specs=in_specs, out_specs=out_specs, check_vma=False)
```

time: 224 us -> 98.4 us (0.44)
  blocking collectives: 95.8 us -> 32.3 us
  local copies, waits for them, and re-layouts: 66.4 us -> 4.36 us
  Pallas kernels: 0 us -> 49 us
  other arithmetic: 33 us -> 0 us
  starting transfers between devices: 17.1 us -> 7.41 us
  matrix products: 7.89 us -> 0 us
  waiting for transfers between devices: 1 us -> 3.99 us
    psum x2 -> x0, blocking collectives: 95.8 us -> none  [the longest x1 63 us: shards(): gram_matrix, live_total = lax.psum((gram_local, live_local), 'row')]
    gather x4 -> x0, local copies, waits for them, and re-layouts: 56 us -> none  [the longest x1 29.2 us: shards(): jnp.take(factor_c, c_local, axis=1).reshape(rank_width, device_count, -1)]
    pallas_call x0 -> x5, Pallas kernels: none -> 49 us  [the longest x1 16.7 us: shards(): pl.pallas_call(functools.partial(weighted_b_kernel, span=span), out_shape...]
    all_to_all x0 -> x2, blocking collectives: none -> 32.3 us  [the longest x1 21.2 us: shards(): lax.all_to_all(payload, 'row', split_axis=0, concat_axis=0, tiled=True)]
    another operation x5 -> x0, other arithmetic: 12.2 us -> none  [the longest x3 6.6 us: shards(): lower_factor = jnp.linalg.cholesky(system)]
    all_to_all x3 -> x1, starting transfers between devices: 17.1 us -> 7.41 us  [shards(): lax.all_to_all(c_out.reshape(devices, pairs // devices, LANES), 'row', sp...]
    transpose x1 -> x0, other arithmetic: 9.6 us -> none  [shards(): weighted_rows = weighted.T]
    select_n x5 -> x0, other arithmetic: 7.46 us -> none  [the longest x1 5.82 us: shards(): jnp.take(factor_c, c_local, axis=1).reshape(rank_width, device_count, -1)]
  transfers between devices with their start and end apart: 3 -> 1, of which waited for: 1 -> 1; matrix products, arithmetic and copies ran while one was open for 32% -> 2% of each run, Pallas kernels for 0% -> 17%
where the time goes in v2:
time: 98.4 us; the launch traced here: 97.8 us
  Pallas kernels  49 us (50%)
  blocking collectives  32.3 us (33%)
  starting transfers between devices  7.41 us (8%)
  local copies, waits for them, and re-layouts  4.36 us (4%)
  waiting for transfers between devices  3.99 us (4%)
    all_to_all x1, blocking collectives, shards(): lax.all_to_all(payload, 'row', split_axis=0, concat_axis=0, tiled=True)  21.2 us
    pallas_call x1, Pallas kernels, shards(): pl.pallas_call(functools.partial(weighted_b_kernel, span=span), out_shape...  16.7 us
    pallas_call x1, Pallas kernels, shards(): pl.pallas_call(functools.partial(outgoing_kernel, span=span), out_shape=s...  15.3 us
    all_to_all x1, blocking collectives, shards(): lax.all_to_all(sums, 'row', split_axis=0, concat_axis=0, tiled=True)  11.2 us
    pallas_call x1, Pallas kernels, shards(): pl.pallas_call(functools.partial(solve_kernel, tiles=tiles, slots=slots,...  7.74 us
    pallas_call x1, Pallas kernels, shards(): pl.pallas_call(functools.partial(sketch_kernel, span=span), out_shape=sha...  7.5 us
    all_to_all x1, starting transfers between devices, shards(): lax.all_to_all(c_out.reshape(devices, pairs // devices, LANES), 'row', sp...  7.41 us
    all_to_all x1, waiting for transfers between devices, shards(): lax.all_to_all(c_out.reshape(devices, pairs // devices, LANES), 'row', sp...  3.99 us
  transfers between devices with their start and end apart: 1, of which 1 were waited for; matrix products, arithmetic and copies ran while one was open for 2% of the time, Pallas kernels for 17%

profile of v2, /device:TPU:0, one launch (start us, length us, event | category | flops | bytes accessed | tf_op | source)
XLA Modules:
  0.0 97.8 jit_solution(16619565689063758937)
XLA Ops:
  0.6 0.0 copy-start.2
  0.6 0.0 copy-start.3
  0.7 0.0 copy-start.1
  0.7 15.3 %outgoing.1 = bf16[4096,128]{1,0:T(8,128)(2,1)} custom-call(s32[1]{0:T(128)} %bitcast.base_ref, s32[8192]{0:T(1024)} %bitcast.10, bf16[64,4096]{1,0:T(8,128)(2,1)} %factor_ref.3), custom_call_target="tpu_custom_call" | custom-call | tf_op jit(solution)/shard_map/outgoing/pallas_call | solution.py:202
  16.0 7.4 %all-to-all-start = ((bf16[16,256,128]{2,1,0:T(8,128)(2,1)}), bf16[16,256,128]{2,1,0:T(8,128)(2,1)S(1)}, u32[]{:S(2)}, u32[]{:S(2)}) async-start(bf16[16,256,128]{2,1,0:T(8,128)(2,1)} %bitcast.8), calls=%async_computation | async-start | bytes 2097152 | tf_op jit(solution)/shard_map/all_to_all | solution.py:213
  23.4 0.0 copy-done.2
  23.4 0.1 copy.10
  23.6 0.7 reshape.25.sample_ref
  24.2 0.0 copy-done.3
  24.2 0.1 copy.11
  24.3 0.7 reshape.26.count_ref
  25.0 0.0 copy-done.1
  25.0 0.6 reshape.27.weight_ref
  25.6 16.7 %weighted_b.1.wb_ref = f32[4096,128]{1,0:T(8,128)} custom-call(s32[1]{0:T(128)} %bitcast.base_ref, s32[8192]{0:T(1024)} %index_ref.1, f32[32,256]{1,0:T(8,128)} %reshape.27.weight_ref, bf16[64,4096]{1,0:T(8,128)(2,1)} %factor_ref.2), custom_call_target="tpu_custom_call" | custom-call | tf_op jit(solution)/shard_map/weighted_b/pallas_call | solution.py:216
  42.3 4.0 %all-to-all-done = bf16[16,256,128]{2,1,0:T(8,128)(2,1)S(1)} async-done(((bf16[16,256,128]{2,1,0:T(8,128)(2,1)}), bf16[16,256,128]{2,1,0:T(8,128)(2,1)S(1)}, u32[]{:S(2)}, u32[]{:S(2)}) %all-to-all-start) | async-done | bytes 1048608 | tf_op jit(solution)/shard_map/all_to_all | solution.py:213
  46.3 0.0 copy-start
  46.3 1.0 %copy-done = bf16[16,256,128]{2,1,0:T(8,128)(2,1)} copy-done((bf16[16,256,128]{2,1,0:T(8,128)(2,1)}, bf16[16,256,128]{2,1,0:T(8,128)(2,1)S(1)}, u32[]{:S(2)}) %copy-start) | copy-done | bytes 1048600
  47.3 7.5 %sketch.1 = f32[16,64,128]{2,1,0:T(8,128)} custom-call(s32[256]{0:T(256)} %reshape.25.sample_ref, s32[256]{0:T(256)} %reshape.26.count_ref, f32[8192]{0:T(1024)} %weight_ref.1, f32[4096,128]{1,0:T(8,128)} %weighted_b.1.wb_ref, bf16[4096,128]{1,0:T(8,128)(2,1)} %bitcast.7, bf16[256,128]{1,0:T(8,128)(2,1)} %bitcast.9), custom_call_target="tpu_custom_call" | custom-call | tf_op jit(solution)/shard_map/sketch/pallas_call | solution.py:225
  54.8 21.2 %all_to_all.15.in_ref = f32[16,64,128]{2,1,0:T(8,128)} all-to-all(f32[16,64,128]{2,1,0:T(8,128)} %sketch.1), channel_id=1, replica_groups=mesh['groups'=2,'row'=16] {'row'}, dimensions={0} | all-to-all | bytes 1048576 | tf_op jit(solution)/shard_map/all_to_all | solution.py:243
  76.0 7.7 %solve.1 = (f32[64,512]{1,0:T(8,128)}, f32[16,8,128]{2,1,0:T(8,128)}) custom-call(f32[16,64,128]{2,1,0:T(8,128)} %all_to_all.15.in_ref), custom_call_target="tpu_custom_call" | custom-call | tf_op jit(solution)/shard_map/solve/pallas_call | solution.py:245
  83.7 11.2 %all_to_all.16.sums_ref = f32[16,8,128]{2,1,0:T(8,128)} all-to-all(f32[16,8,128]{2,1,0:T(8,128)} %get-tuple-element.6), channel_id=1, replica_groups=mesh['groups'=2,'row'=16] {'row'}, dimensions={0} | all-to-all | bytes 131072 | tf_op jit(solution)/shard_map/all_to_all | solution.py:258
  94.9 1.8 %scale.1 = (bf16[64,512]{1,0:T(8,128)(2,1)}, f32[8,128]{1,0:T(8,128)}) custom-call(f32[16,8,128]{2,1,0:T(8,128)} %all_to_all.16.sums_ref, f32[64,512]{1,0:T(8,128)} %get-tuple-element.7.update_ref), custom_call_target="tpu_custom_call" | custom-call | tf_op jit(solution)/shard_map/scale/pallas_call | solution.py:259
  96.6 1.2 %slice_bitcast_fusion = f32[64]{0:T(128)} fusion(f32[8,128]{1,0:T(8,128)} %get-tuple-element.9), kind=kLoop, calls=%fused_computation | loop fusion | bytes 512 | tf_op jit(solution)/shard_map/squeeze | solution.py:266
Async XLA Ops:
  0.6 22.8 %copy-start.2 = (s32[1,16,4,4]{1,3,2,0:T(4,128)S(1)}, s32[1,16,4,4]{1,3,2,0:T(4,128)}, u32[]{:S(2)}) copy-start(s32[1,16,4,4]{1,3,2,0:T(4,128)} %param.14) | copy-start | bytes 3076
  0.6 23.6 %copy-start.3 = (s32[1,16,4,4]{1,3,2,0:T(4,128)S(1)}, s32[1,16,4,4]{1,3,2,0:T(4,128)}, u32[]{:S(2)}) copy-start(s32[1,16,4,4]{1,3,2,0:T(4,128)} %param.15) | copy-start | bytes 3076
  0.7 24.4 %copy-start.1 = (f32[8192]{0:T(1024)S(1)}, f32[8192]{0:T(1024)}, u32[]{:S(2)}) copy-start(f32[8192]{0:T(1024)} %weight_ref.1) | copy-start | bytes 98308
  16.0 30.3 %all-to-all-start = ((bf16[16,256,128]{2,1,0:T(8,128)(2,1)}), bf16[16,256,128]{2,1,0:T(8,128)(2,1)S(1)}, u32[]{:S(2)}, u32[]{:S(2)}) async-start(bf16[16,256,128]{2,1,0:T(8,128)(2,1)} %bitcast.8), calls=%async_computation | async-start | bytes 2097152 | tf_op jit(solution)/shard_map/all_to_all | solution.py:213
  46.3 1.0 %copy-start = (bf16[16,256,128]{2,1,0:T(8,128)(2,1)}, bf16[16,256,128]{2,1,0:T(8,128)(2,1)S(1)}, u32[]{:S(2)}) copy-start(bf16[16,256,128]{2,1,0:T(8,128)(2,1)S(1)} %all-to-all-done) | copy-start | bytes 3145732

commit v3 on v2

--- a/solution.py
+++ b/solution.py
@@ -30,18 +30,26 @@
     lax.fori_loop(0, columns // LANES, step, 0)
 
 
-def gather_pairs(base_ref, index_ref, table_ref, rows_ref, span):
+def start_indices(base_ref, index_ref, local_ref, scalar_ref, sem):
+    local_ref[...] = index_ref[...] - base_ref[0]
+    copy = pltpu.make_async_copy(local_ref, scalar_ref, sem)
+    copy.start()
+    return copy
+
+
+def gather_pairs(scalar_ref, table_ref, rows_ref, span):
     half = span // 2
-    step_rows = min(32, half)
+    step_rows = min(LANES, half)
     low = lane_index((1, LANES)) < LANES // 2
-    base = base_ref[0]
 
     def step(q, carry):
-        row = q * step_rows
+        row = pl.multiple_of(q * step_rows, step_rows)
         first = row + lax.div(row, half) * half
+        index_row = lax.div(first, LANES)
         for u in range(step_rows):
-            a = index_ref[first + u] - base
-            b = index_ref[first + (u + half)] - base
+            ahead, column = divmod(u + half, LANES)
+            a = scalar_ref[index_row, u]
+            b = scalar_ref[index_row + ahead, column]
             rows_ref[pl.ds(row + u, 1), :] = jnp.where(
                 low, table_ref[pl.ds(a, 1), :], table_ref[pl.ds(b, 1), :]
             )
@@ -50,25 +58,46 @@
     lax.fori_loop(0, rows_ref.shape[0] // step_rows, step, 0)
 
 
-def outgoing_kernel(base_ref, index_ref, factor_ref, out_ref, table_ref, rows_ref, *, span):
+def outgoing_kernel(
+    base_ref, index_ref, factor_ref, out_ref, table_ref, rows_ref, local_ref, scalar_ref, sem, *, span
+):
+    copy = start_indices(base_ref, index_ref, local_ref, scalar_ref, sem)
     fill_table(factor_ref, table_ref)
-    gather_pairs(base_ref, index_ref, table_ref, rows_ref, span)
+    copy.wait()
+    gather_pairs(scalar_ref, table_ref, rows_ref, span)
     out_ref[...] = rows_ref[...].astype(jnp.bfloat16)
 
 
-def weighted_b_kernel(base_ref, index_ref, weight_ref, factor_ref, out_ref, table_ref, *, span):
+def weighted_b_kernel(
+    base_ref, count_ref, index_ref, weight_ref, factor_ref, values_ref,
+    out_ref, masked_ref, table_ref, local_ref, scalar_ref, sem, *, span
+):
     half = span // 2
+    copy = start_indices(base_ref, index_ref, local_ref, scalar_ref, sem)
     fill_table(factor_ref, table_ref)
-    gather_pairs(base_ref, index_ref, table_ref, out_ref, span)
+    copy.wait()
+    gather_pairs(scalar_ref, table_ref, out_ref, span)
     turned = weight_ref[...].T
     low = lane_index((half, LANES)) < LANES // 2
     for e in range(out_ref.shape[0] // half):
         weights = jnp.where(low, turned[:, 2 * e : 2 * e + 1], turned[:, 2 * e + 1 : 2 * e + 2])
         out_ref[e * half : (e + 1) * half, :] = out_ref[e * half : (e + 1) * half, :] * weights
+    masked_ref[...] = values_ref[...].astype(jnp.float32)
+    lane = lane_index((1, LANES))
+    step_rows = 16
+
+    def mask_step(q, carry):
+        row = pl.multiple_of(q * step_rows, step_rows)
+        for u in range(step_rows):
+            value_row = masked_ref[pl.ds(row + u, 1), :]
+            masked_ref[pl.ds(row + u, 1), :] = jnp.where(lane < count_ref[row + u], value_row, 0.0)
+        return carry
+
+    lax.fori_loop(0, values_ref.shape[0] // step_rows, mask_step, 0)
 
 
 def sketch_kernel(
-    sample_ref, count_ref, weight_ref, wb_ref, c_ref, values_ref, out_ref, sketch_ref, values32_ref, *, span
+    sample_ref, count_ref, weight_ref, wb_ref, c_ref, values_ref, out_ref, sketch_ref, *, span
 ):
     half = span // 2
     total_rows = wb_ref.shape[0]
@@ -94,8 +123,6 @@
     gram = full[:rank] + pltpu.roll(full[rank:], rank, 1)
     low = lane_index((1, LANES)) < rank
     packed = jnp.where(low, gram[: rank // 2], pltpu.roll(gram[rank // 2 :], rank, 1))
-    lane = lane_index((1, LANES))
-    values32_ref[...] = values_ref[...].astype(jnp.float32)
 
     def count_step(q, total):
         for u in range(blocks):
@@ -116,8 +143,7 @@
             picked = jnp.where(upper, pltpu.roll(scaled, rank, 1), scaled)
             rounded = picked.astype(jnp.bfloat16).astype(jnp.float32)
             out_ref[q, blocks + u : blocks + u + 1, :] = jnp.where(low, rounded, live)
-            value_row = values32_ref[pl.ds(j, 1), :]
-            out_ref[q, u : u + 1, :] = jnp.where(lane < count_ref[j], value_row, 0.0)
+        out_ref[q, :blocks, :] = values_ref[pl.ds(pl.multiple_of(q * blocks, blocks), blocks), :]
         out_ref[q, 2 * blocks :, :] = packed
         return carry
 
@@ -176,7 +202,7 @@
     for p in range(1, sums_ref.shape[0]):
         summed = summed + sums_ref[p]
     scales = jnp.sqrt(summed / total_rows + 1e-06)
-    scales_ref[...] = scales
+    scales_ref[...] = scales[0:1, :rank]
     column = jnp.broadcast_to(scales[0:1], (LANES, LANES)).T[:rank, 0:1]
     out_ref[...] = (update_ref[...] / column).astype(jnp.bfloat16)
 
@@ -199,47 +225,52 @@
     f32 = jnp.float32
     c_base = jnp.full((1,), position * factor_c.shape[1], jnp.int32)
     b_base = jnp.full((1,), position * factor_b.shape[1], jnp.int32)
+    index_shape = (samples // LANES, LANES)
+    index_scratch = [
+        pltpu.VMEM(index_shape, jnp.int32),
+        pltpu.SMEM(index_shape, jnp.int32),
+        pltpu.SemaphoreType.DMA,
+    ]
+    blocks = tiles * slots
+    counts = block_count.reshape(-1)
     c_out = pl.pallas_call(
         functools.partial(outgoing_kernel, span=span),
         out_shape=shape((pairs, LANES), jnp.bfloat16),
-        in_specs=[SMEM, SMEM, VMEM],
+        in_specs=[SMEM, VMEM, VMEM],
         out_specs=VMEM,
         scratch_shapes=[
             pltpu.VMEM((factor_c.shape[1], LANES), f32),
             pltpu.VMEM((pairs, LANES), f32),
+            *index_scratch,
         ],
         name="outgoing",
-    )(c_base, sample_k.reshape(-1), factor_c)
+    )(c_base, sample_k.reshape(index_shape), factor_c)
     c_in = lax.all_to_all(
         c_out.reshape(devices, pairs // devices, LANES), "row", split_axis=0, concat_axis=0, tiled=True
     ).reshape(pairs, LANES)
-    weighted_b = pl.pallas_call(
+    weighted_b, masked = pl.pallas_call(
         functools.partial(weighted_b_kernel, span=span),
-        out_shape=shape((pairs, LANES), f32),
-        in_specs=[SMEM, SMEM, VMEM, VMEM],
-        out_specs=VMEM,
-        scratch_shapes=[pltpu.VMEM((factor_b.shape[1], LANES), f32)],
+        out_shape=(shape((pairs, LANES), f32), shape((devices * blocks, LANES), f32)),
+        in_specs=[SMEM, SMEM, VMEM, VMEM, VMEM, VMEM],
+        out_specs=(VMEM, VMEM),
+        scratch_shapes=[pltpu.VMEM((factor_b.shape[1], LANES), f32), *index_scratch],
         name="weighted_b",
-    )(b_base, sample_j, sample_weight.reshape(2 * devices, span // 2), factor_b)
-    blocks = tiles * slots
+    )(
+        b_base,
+        counts,
+        sample_j.reshape(index_shape),
+        sample_weight.reshape(2 * devices, span // 2),
+        factor_b,
+        block_values.reshape(devices * blocks, LANES),
+    )
     payload = pl.pallas_call(
         functools.partial(sketch_kernel, span=span),
         out_shape=shape((devices, 2 * blocks + rank // 2, LANES), f32),
         in_specs=[SMEM, SMEM, SMEM, VMEM, VMEM, VMEM],
         out_specs=VMEM,
-        scratch_shapes=[
-            pltpu.VMEM((pairs, LANES), f32),
-            pltpu.VMEM((devices * blocks, LANES), f32),
-        ],
+        scratch_shapes=[pltpu.VMEM((pairs, LANES), f32)],
         name="sketch",
-    )(
-        block_sample.reshape(-1),
-        block_count.reshape(-1),
-        sample_weight,
-        weighted_b,
-        c_in,
-        block_values.reshape(devices * blocks, LANES),
-    )
+    )(block_sample.reshape(-1), counts, sample_weight, weighted_b, c_in, masked)
     received = lax.all_to_all(payload, "row", split_axis=0, concat_axis=0, tiled=True)
     total_rows = tiles * LANES * devices
     update, sums = pl.pallas_call(
@@ -258,12 +289,12 @@
     all_sums = lax.all_to_all(sums, "row", split_axis=0, concat_axis=0, tiled=True)
     factor_new, scales = pl.pallas_call(
         functools.partial(scale_kernel, total_rows=total_rows),
-        out_shape=(shape((rank, tiles * LANES), jnp.bfloat16), shape((8, LANES), f32)),
+        out_shape=(shape((rank, tiles * LANES), jnp.bfloat16), shape((1, rank), f32)),
         in_specs=[VMEM, VMEM],
         out_specs=(VMEM, VMEM),
         name="scale",
     )(all_sums, update)
-    return factor_new, scales[0, :rank]
+    return factor_new, scales.reshape(rank)
 
 
 def solution(mesh):

time: 98.4 us -> 93.9 us (0.954)
  Pallas kernels: 49 us -> 43.1 us
  waiting for transfers between devices: 3.99 us -> 6.65 us
  local copies, waits for them, and re-layouts: 4.36 us -> 3.18 us
    pallas_call x1, Pallas kernels: 15.3 us -> 12.3 us  [shards(): pl.pallas_call(functools.partial(outgoing_kernel, span=span), out_shape=s...]
    pallas_call x1, Pallas kernels: 16.7 us -> 14 us  [shards(): pl.pallas_call(functools.partial(weighted_b_kernel, span=span), out_shape...]
    all_to_all x1, waiting for transfers between devices: 3.99 us -> 6.65 us  [shards(): lax.all_to_all(c_out.reshape(devices, pairs // devices, LANES), 'row', sp...]
    squeeze x1 -> x0, local copies, waits for them, and re-layouts: 1.18 us -> none  [shards(): return (factor_new, scales[0, :rank])]
  transfers between devices with their start and end apart: 1 -> 1, of which waited for: 1 -> 1; matrix products, arithmetic and copies ran while one was open for 2% -> 2% of each run, Pallas kernels for 17% -> 15%
where the time goes in v3:
time: 93.9 us; the launch traced here: 93.4 us
  Pallas kernels  43.1 us (46%)
  blocking collectives  32.3 us (34%)
  starting transfers between devices  7.43 us (8%)
  waiting for transfers between devices  6.65 us (7%)
  local copies, waits for them, and re-layouts  3.18 us (3%)
    all_to_all x1, blocking collectives, shards(): lax.all_to_all(payload, 'row', split_axis=0, concat_axis=0, tiled=True)  21.2 us
    pallas_call x1, Pallas kernels, shards(): pl.pallas_call(functools.partial(weighted_b_kernel, span=span), out_shape...  14 us
    pallas_call x1, Pallas kernels, shards(): pl.pallas_call(functools.partial(outgoing_kernel, span=span), out_shape=s...  12.3 us
    all_to_all x1, blocking collectives, shards(): lax.all_to_all(sums, 'row', split_axis=0, concat_axis=0, tiled=True)  11.2 us
    pallas_call x1, Pallas kernels, shards(): pl.pallas_call(functools.partial(solve_kernel, tiles=tiles, slots=slots,...  7.75 us
    all_to_all x1, starting transfers between devices, shards(): lax.all_to_all(c_out.reshape(devices, pairs // devices, LANES), 'row', sp...  7.43 us
    pallas_call x1, Pallas kernels, shards(): pl.pallas_call(functools.partial(sketch_kernel, span=span), out_shape=sha...  7.32 us
    all_to_all x1, waiting for transfers between devices, shards(): lax.all_to_all(c_out.reshape(devices, pairs // devices, LANES), 'row', sp...  6.65 us
  transfers between devices with their start and end apart: 1, of which 1 were waited for; matrix products, arithmetic and copies ran while one was open for 2% of the time, Pallas kernels for 15%

profile of v3, /device:TPU:0, one launch (start us, length us, event | category | flops | bytes accessed | tf_op | source)
XLA Modules:
  0.0 93.4 jit_solution(4879007544326103774)
XLA Ops:
  0.6 0.0 copy-start.2
  0.6 0.0 copy-start.3
  0.7 0.0 copy-start.1
  0.7 12.3 %outgoing.1 = bf16[4096,128]{1,0:T(8,128)(2,1)} custom-call(s32[1]{0:T(128)} %bitcast.base_ref, s32[64,128]{1,0:T(8,128)} %bitcast.10, bf16[64,4096]{1,0:T(8,128)(2,1)} %factor_ref.3), custom_call_target="tpu_custom_call" | custom-call | tf_op jit(solution)/shard_map/outgoing/pallas_call | solution.py:236
  12.9 7.4 %all-to-all-start = ((bf16[16,256,128]{2,1,0:T(8,128)(2,1)}), bf16[16,256,128]{2,1,0:T(8,128)(2,1)S(1)}, u32[]{:S(2)}, u32[]{:S(2)}) async-start(bf16[16,256,128]{2,1,0:T(8,128)(2,1)} %bitcast.8), calls=%async_computation | async-start | bytes 2097152 | tf_op jit(solution)/shard_map/all_to_all | solution.py:248
  20.4 0.0 copy-done.2
  20.4 0.1 copy.10
  20.5 0.7 reshape.31.sample_ref
  21.1 0.0 copy-done.3
  21.1 0.1 copy.11
  21.2 0.7 reshape.32.count_ref
  21.9 0.0 copy-done.1
  21.9 0.6 reshape.34.weight_ref
  22.6 14.0 %weighted_b.1 = (f32[4096,128]{1,0:T(8,128)}, f32[256,128]{1,0:T(8,128)}) custom-call(s32[1]{0:T(128)} %bitcast.base_ref, s32[256]{0:T(256)} %reshape.32.count_ref, s32[64,128]{1,0:T(8,128)} %bitcast.11, f32[32,256]{1,0:T(8,128)} %reshape.34.weight_ref, bf16[64,4096]{1,0:T(8,128)(2,1)} %factor_ref.2, bf16[256,128]{1,0:T(8,128)(2,1)} %bitcast.9), custom_call_target="tpu_custom_call" | custom-call | tf_op jit(solution)/shard_map/weighted_b/pallas_call | solution.py:251
  36.6 6.6 %all-to-all-done = bf16[16,256,128]{2,1,0:T(8,128)(2,1)S(1)} async-done(((bf16[16,256,128]{2,1,0:T(8,128)(2,1)}), bf16[16,256,128]{2,1,0:T(8,128)(2,1)S(1)}, u32[]{:S(2)}, u32[]{:S(2)}) %all-to-all-start) | async-done | bytes 1048608 | tf_op jit(solution)/shard_map/all_to_all | solution.py:248
  43.2 0.0 copy-start
  43.3 1.0 %copy-done = bf16[16,256,128]{2,1,0:T(8,128)(2,1)} copy-done((bf16[16,256,128]{2,1,0:T(8,128)(2,1)}, bf16[16,256,128]{2,1,0:T(8,128)(2,1)S(1)}, u32[]{:S(2)}) %copy-start) | copy-done | bytes 1048600
  44.2 7.3 %sketch.1 = f32[16,64,128]{2,1,0:T(8,128)} custom-call(s32[256]{0:T(256)} %reshape.31.sample_ref, s32[256]{0:T(256)} %reshape.32.count_ref, f32[8192]{0:T(1024)} %weight_ref.1, f32[4096,128]{1,0:T(8,128)} %get-tuple-element.8.wb_ref, bf16[4096,128]{1,0:T(8,128)(2,1)} %bitcast.7, f32[256,128]{1,0:T(8,128)} %get-tuple-element.9.values_ref), custom_call_target="tpu_custom_call" | custom-call | tf_op jit(solution)/shard_map/sketch/pallas_call | solution.py:266
  51.6 21.2 %all_to_all.15.in_ref = f32[16,64,128]{2,1,0:T(8,128)} all-to-all(f32[16,64,128]{2,1,0:T(8,128)} %sketch.1), channel_id=1, replica_groups=mesh['groups'=2,'row'=16] {'row'}, dimensions={0} | all-to-all | bytes 1048576 | tf_op jit(solution)/shard_map/all_to_all | solution.py:274
  72.7 7.7 %solve.1 = (f32[64,512]{1,0:T(8,128)}, f32[16,8,128]{2,1,0:T(8,128)}) custom-call(f32[16,64,128]{2,1,0:T(8,128)} %all_to_all.15.in_ref), custom_call_target="tpu_custom_call" | custom-call | tf_op jit(solution)/shard_map/solve/pallas_call | solution.py:276
  80.5 11.2 %all_to_all.16.sums_ref = f32[16,8,128]{2,1,0:T(8,128)} all-to-all(f32[16,8,128]{2,1,0:T(8,128)} %get-tuple-element.10), channel_id=1, replica_groups=mesh['groups'=2,'row'=16] {'row'}, dimensions={0} | all-to-all | bytes 131072 | tf_op jit(solution)/shard_map/all_to_all | solution.py:289
  91.6 1.8 %scale.1 = (bf16[64,512]{1,0:T(8,128)(2,1)}, f32[1,64]{1,0:T(1,128)}) custom-call(f32[16,8,128]{2,1,0:T(8,128)} %all_to_all.16.sums_ref, f32[64,512]{1,0:T(8,128)} %get-tuple-element.11.update_ref), custom_call_target="tpu_custom_call" | custom-call | tf_op jit(solution)/shard_map/scale/pallas_call | solution.py:290
Async XLA Ops:
  0.6 19.7 %copy-start.2 = (s32[1,16,4,4]{1,3,2,0:T(4,128)S(1)}, s32[1,16,4,4]{1,3,2,0:T(4,128)}, u32[]{:S(2)}) copy-start(s32[1,16,4,4]{1,3,2,0:T(4,128)} %param.14) | copy-start | bytes 3076
  0.6 20.5 %copy-start.3 = (s32[1,16,4,4]{1,3,2,0:T(4,128)S(1)}, s32[1,16,4,4]{1,3,2,0:T(4,128)}, u32[]{:S(2)}) copy-start(s32[1,16,4,4]{1,3,2,0:T(4,128)} %param.15) | copy-start | bytes 3076
  0.7 21.3 %copy-start.1 = (f32[8192]{0:T(1024)S(1)}, f32[8192]{0:T(1024)}, u32[]{:S(2)}) copy-start(f32[8192]{0:T(1024)} %weight_ref.1) | copy-start | bytes 98308
  12.9 30.3 %all-to-all-start = ((bf16[16,256,128]{2,1,0:T(8,128)(2,1)}), bf16[16,256,128]{2,1,0:T(8,128)(2,1)S(1)}, u32[]{:S(2)}, u32[]{:S(2)}) async-start(bf16[16,256,128]{2,1,0:T(8,128)(2,1)} %bitcast.8), calls=%async_computation | async-start | bytes 2097152 | tf_op jit(solution)/shard_map/all_to_all | solution.py:248
  43.2 1.0 %copy-start = (bf16[16,256,128]{2,1,0:T(8,128)(2,1)}, bf16[16,256,128]{2,1,0:T(8,128)(2,1)S(1)}, u32[]{:S(2)}) copy-start(bf16[16,256,128]{2,1,0:T(8,128)(2,1)S(1)} %all-to-all-done) | copy-start | bytes 3145732

commit v4 on v3

--- a/solution.py
+++ b/solution.py
@@ -70,7 +70,7 @@
 
 def weighted_b_kernel(
     base_ref, count_ref, index_ref, weight_ref, factor_ref, values_ref,
-    out_ref, masked_ref, table_ref, local_ref, scalar_ref, sem, *, span
+    out_ref, masked_ref, table_ref, local_ref, scalar_ref, sem, wide_ref, *, span
 ):
     half = span // 2
     copy = start_indices(base_ref, index_ref, local_ref, scalar_ref, sem)
@@ -82,22 +82,28 @@
     for e in range(out_ref.shape[0] // half):
         weights = jnp.where(low, turned[:, 2 * e : 2 * e + 1], turned[:, 2 * e + 1 : 2 * e + 2])
         out_ref[e * half : (e + 1) * half, :] = out_ref[e * half : (e + 1) * half, :] * weights
-    masked_ref[...] = values_ref[...].astype(jnp.float32)
+    wide_ref[...] = values_ref[...].astype(jnp.float32)
     lane = lane_index((1, LANES))
     step_rows = 16
 
     def mask_step(q, carry):
         row = pl.multiple_of(q * step_rows, step_rows)
         for u in range(step_rows):
-            value_row = masked_ref[pl.ds(row + u, 1), :]
-            masked_ref[pl.ds(row + u, 1), :] = jnp.where(lane < count_ref[row + u], value_row, 0.0)
+            value_row = wide_ref[pl.ds(row + u, 1), :]
+            wide_ref[pl.ds(row + u, 1), :] = jnp.where(lane < count_ref[row + u], value_row, 0.0)
         return carry
 
     lax.fori_loop(0, values_ref.shape[0] // step_rows, mask_step, 0)
+    masked_ref[...] = wide_ref[...].astype(jnp.bfloat16)
+
+
+def split(x):
+    high = x.astype(jnp.bfloat16).astype(jnp.float32)
+    return high, x - high
 
 
 def sketch_kernel(
-    sample_ref, count_ref, weight_ref, wb_ref, c_ref, values_ref, out_ref, sketch_ref, *, span
+    sample_ref, count_ref, weight_ref, wb_ref, c_ref, values_ref, out_ref, sketch_ref, picked_ref, *, span
 ):
     half = span // 2
     total_rows = wb_ref.shape[0]
@@ -122,7 +128,17 @@
     full = acc[:, :LANES] + cross + cross.T
     gram = full[:rank] + pltpu.roll(full[rank:], rank, 1)
     low = lane_index((1, LANES)) < rank
-    packed = jnp.where(low, gram[: rank // 2], pltpu.roll(gram[rank // 2 :], rank, 1))
+    quarter = rank // 2
+    lane = lane_index((quarter, LANES))
+    sub = lax.broadcasted_iota(jnp.int32, (quarter, LANES), 0)
+    top, bottom = gram[:quarter], gram[quarter:]
+    folded = jnp.where(lane < jnp.minimum(sub, quarter), pltpu.roll(bottom, LANES - quarter, 1), top)
+    high, rest = split(folded)
+    packed = jnp.where(low, high, pltpu.roll(rest, rank, 1)).astype(jnp.bfloat16)
+    diagonal = jnp.sum(jnp.where(lane == sub + quarter, bottom, 0.0), axis=0, keepdims=True)
+    high, rest = split(diagonal)
+    third = lane_index((1, LANES)) < rank + quarter
+    diagonal_row = jnp.where(third, pltpu.roll(high, quarter, 1), pltpu.roll(rest, rank, 1))
 
     def count_step(q, total):
         for u in range(blocks):
@@ -130,6 +146,8 @@
         return total
 
     live = lax.fori_loop(0, devices, count_step, jnp.int32(0)).astype(jnp.float32)
+    high, rest = split(jnp.full((1, LANES), live, jnp.float32))
+    spare = [diagonal_row, jnp.where(third, high, rest)]
 
     def pick_step(q, carry):
         for u in range(blocks):
@@ -141,9 +159,9 @@
             row = e * half + jnp.where(upper, i - half, i)
             scaled = sketch_ref[pl.ds(row, 1), :] * weight_ref[s]
             picked = jnp.where(upper, pltpu.roll(scaled, rank, 1), scaled)
-            rounded = picked.astype(jnp.bfloat16).astype(jnp.float32)
-            out_ref[q, blocks + u : blocks + u + 1, :] = jnp.where(low, rounded, live)
+            picked_ref[q, u : u + 1, :] = jnp.where(low, picked, spare[u]) if u < 2 else picked
         out_ref[q, :blocks, :] = values_ref[pl.ds(pl.multiple_of(q * blocks, blocks), blocks), :]
+        out_ref[q, blocks : 2 * blocks, :] = picked_ref[q].astype(jnp.bfloat16)
         out_ref[q, 2 * blocks :, :] = packed
         return carry
 
@@ -154,13 +172,26 @@
     devices = in_ref.shape[0]
     rank = LANES // 2
     blocks = tiles * slots
-    summed = in_ref[0, 2 * blocks :, :]
-    live_row = in_ref[0, blocks : blocks + 1, :]
+    f32 = jnp.float32
+    summed = in_ref[0, 2 * blocks :, :].astype(f32)
+    spare = in_ref[0, blocks : 2 * blocks, :].astype(f32)
     for p in range(1, devices):
-        summed = summed + in_ref[p, 2 * blocks :, :]
-        live_row = live_row + in_ref[p, blocks : blocks + 1, :]
-    gram = jnp.concatenate([summed, pltpu.roll(summed, rank, 1)], axis=0)
-    ridge = 0.05 * pltpu.roll(live_row, rank, 1)[:, 0:1] / total_rows
+        summed = summed + in_ref[p, 2 * blocks :, :].astype(f32)
+        spare = spare + in_ref[p, blocks : 2 * blocks, :].astype(f32)
+    quarter = rank // 2
+    lane = lane_index((quarter, LANES))
+    sub = lax.broadcasted_iota(jnp.int32, (quarter, LANES), 0)
+    folded = summed + pltpu.roll(summed, rank, 1)
+    joined = spare[0:8] + pltpu.roll(spare[0:8], LANES - quarter, 1)
+    joined = pltpu.roll(joined, rank, 1)
+    turned = jnp.concatenate([folded] + [jnp.zeros_like(folded)] * 3, axis=0).T
+    mirror = turned[:quarter]
+    first = jnp.where(lane < sub, mirror, folded)
+    first = jnp.where(lane < quarter, first, folded)
+    last = jnp.where(lane < sub, folded, jnp.where(lane > sub, mirror, joined[0:1]))
+    last = jnp.where(lane < quarter, turned[quarter:rank], pltpu.roll(last, quarter, 1))
+    gram = jnp.concatenate([first, last], axis=0)
+    ridge = 0.05 * joined[1:2, 0:1] / total_rows
     lane = lane_index((rank, LANES))
     sub = lax.broadcasted_iota(jnp.int32, (rank, LANES), 0)
     state = gram / total_samples + jnp.where(lane == sub, ridge, 0.0)
@@ -172,8 +203,8 @@
         rest = jnp.where(lane == k, 0.0, state)
         state = jnp.where(sub == k, row, rest - column * row)
     inverse = state[:, :rank]
-    values = in_ref[:, :blocks, :].reshape(devices * blocks, LANES).astype(jnp.bfloat16)
-    rows = in_ref[:, blocks : 2 * blocks, :].reshape(devices * blocks, LANES)
+    values = in_ref[:, :blocks, :].reshape(devices * blocks, LANES)
+    rows = in_ref[:, blocks : 2 * blocks, :].reshape(devices * blocks, LANES).astype(f32)
     wide = lane_index(rows.shape)
     doubled = jnp.where(wide < rank, rows, pltpu.roll(rows, rank, 1))
     tile_of = lax.div(
@@ -250,10 +281,14 @@
     ).reshape(pairs, LANES)
     weighted_b, masked = pl.pallas_call(
         functools.partial(weighted_b_kernel, span=span),
-        out_shape=(shape((pairs, LANES), f32), shape((devices * blocks, LANES), f32)),
+        out_shape=(shape((pairs, LANES), f32), shape((devices * blocks, LANES), jnp.bfloat16)),
         in_specs=[SMEM, SMEM, VMEM, VMEM, VMEM, VMEM],
         out_specs=(VMEM, VMEM),
-        scratch_shapes=[pltpu.VMEM((factor_b.shape[1], LANES), f32), *index_scratch],
+        scratch_shapes=[
+            pltpu.VMEM((factor_b.shape[1], LANES), f32),
+            *index_scratch,
+            pltpu.VMEM((devices * blocks, LANES), f32),
+        ],
         name="weighted_b",
     )(
         b_base,
@@ -265,10 +300,13 @@
     )
     payload = pl.pallas_call(
         functools.partial(sketch_kernel, span=span),
-        out_shape=shape((devices, 2 * blocks + rank // 2, LANES), f32),
+        out_shape=shape((devices, 2 * blocks + rank // 2, LANES), jnp.bfloat16),
         in_specs=[SMEM, SMEM, SMEM, VMEM, VMEM, VMEM],
         out_specs=VMEM,
-        scratch_shapes=[pltpu.VMEM((pairs, LANES), f32)],
+        scratch_shapes=[
+            pltpu.VMEM((pairs, LANES), f32),
+            pltpu.VMEM((devices, blocks, LANES), f32),
+        ],
         name="sketch",
     )(block_sample.reshape(-1), counts, sample_weight, weighted_b, c_in, masked)
     received = lax.all_to_all(payload, "row", split_axis=0, concat_axis=0, tiled=True)

time: 93.9 us -> 89.5 us (0.953)
  blocking collectives: 32.3 us -> 28 us
    all_to_all x1, blocking collectives: 21.2 us -> 16.9 us  [shards(): lax.all_to_all(payload, 'row', split_axis=0, concat_axis=0, tiled=True)]
  transfers between devices with their start and end apart: 1 -> 1, of which waited for: 1 -> 1; matrix products, arithmetic and copies ran while one was open for 2% -> 2% of each run, Pallas kernels for 15% -> 16%
where the time goes in v4:
time: 89.5 us; the launch traced here: 89 us
  Pallas kernels  43.1 us (48%)
  blocking collectives  28 us (31%)
  starting transfers between devices  7.43 us (8%)
  waiting for transfers between devices  6.74 us (8%)
  local copies, waits for them, and re-layouts  3.11 us (3%)
    all_to_all x1, blocking collectives, shards(): lax.all_to_all(payload, 'row', split_axis=0, concat_axis=0, tiled=True)  16.9 us
    pallas_call x1, Pallas kernels, shards(): pl.pallas_call(functools.partial(weighted_b_kernel, span=span), out_shape...  14 us
    pallas_call x1, Pallas kernels, shards(): pl.pallas_call(functools.partial(outgoing_kernel, span=span), out_shape=s...  12.3 us
    all_to_all x1, blocking collectives, shards(): lax.all_to_all(sums, 'row', split_axis=0, concat_axis=0, tiled=True)  11 us
    pallas_call x1, Pallas kernels, shards(): pl.pallas_call(functools.partial(solve_kernel, tiles=tiles, slots=slots,...  7.77 us
    all_to_all x1, starting transfers between devices, shards(): lax.all_to_all(c_out.reshape(devices, pairs // devices, LANES), 'row', sp...  7.43 us
    pallas_call x1, Pallas kernels, shards(): pl.pallas_call(functools.partial(sketch_kernel, span=span), out_shape=sha...  7.28 us
    all_to_all x1, waiting for transfers between devices, shards(): lax.all_to_all(c_out.reshape(devices, pairs // devices, LANES), 'row', sp...  6.74 us
  transfers between devices with their start and end apart: 1, of which 1 were waited for; matrix products, arithmetic and copies ran while one was open for 2% of the time, Pallas kernels for 16%

profile of v4, /device:TPU:0, one launch (start us, length us, event | category | flops | bytes accessed | tf_op | source)
XLA Modules:
  0.0 89.0 jit_solution(5423439247753183383)
XLA Ops:
  0.6 0.0 copy-start.2
  0.6 0.0 copy-start.3
  0.7 0.0 copy-start.1
  0.7 12.3 %outgoing.1 = bf16[4096,128]{1,0:T(8,128)(2,1)} custom-call(s32[1]{0:T(128)} %bitcast.base_ref, s32[64,128]{1,0:T(8,128)} %bitcast.10, bf16[64,4096]{1,0:T(8,128)(2,1)} %factor_ref.3), custom_call_target="tpu_custom_call" | custom-call | tf_op jit(solution)/shard_map/outgoing/pallas_call | solution.py:267
  12.9 7.4 %all-to-all-start = ((bf16[16,256,128]{2,1,0:T(8,128)(2,1)}), bf16[16,256,128]{2,1,0:T(8,128)(2,1)S(1)}, u32[]{:S(2)}, u32[]{:S(2)}) async-start(bf16[16,256,128]{2,1,0:T(8,128)(2,1)} %bitcast.8), calls=%async_computation | async-start | bytes 2097152 | tf_op jit(solution)/shard_map/all_to_all | solution.py:279
  20.4 0.0 copy-done.2
  20.4 0.1 copy.10
  20.5 0.6 reshape.31.sample_ref
  21.1 0.0 copy-done.3
  21.1 0.1 copy.11
  21.2 0.6 reshape.32.count_ref
  21.9 0.0 copy-done.1
  21.9 0.6 reshape.34.weight_ref
  22.5 14.0 %weighted_b.1 = (f32[4096,128]{1,0:T(8,128)}, bf16[256,128]{1,0:T(8,128)(2,1)}) custom-call(s32[1]{0:T(128)} %bitcast.base_ref, s32[256]{0:T(256)} %reshape.32.count_ref, s32[64,128]{1,0:T(8,128)} %bitcast.11, f32[32,256]{1,0:T(8,128)} %reshape.34.weight_ref, bf16[64,4096]{1,0:T(8,128)(2,1)} %factor_ref.2, bf16[256,128]{1,0:T(8,128)(2,1)} %bitcast.9), custom_call_target="tpu_custom_call" | custom-call | tf_op jit(solution)/shard_map/weighted_b/pallas_call | solution.py:282
  36.5 6.7 %all-to-all-done = bf16[16,256,128]{2,1,0:T(8,128)(2,1)S(1)} async-done(((bf16[16,256,128]{2,1,0:T(8,128)(2,1)}), bf16[16,256,128]{2,1,0:T(8,128)(2,1)S(1)}, u32[]{:S(2)}, u32[]{:S(2)}) %all-to-all-start) | async-done | bytes 1048608 | tf_op jit(solution)/shard_map/all_to_all | solution.py:279
  43.2 0.0 copy-start
  43.3 1.0 %copy-done = bf16[16,256,128]{2,1,0:T(8,128)(2,1)} copy-done((bf16[16,256,128]{2,1,0:T(8,128)(2,1)}, bf16[16,256,128]{2,1,0:T(8,128)(2,1)S(1)}, u32[]{:S(2)}) %copy-start) | copy-done | bytes 1048600
  44.2 7.3 %sketch.1 = bf16[16,64,128]{2,1,0:T(8,128)(2,1)} custom-call(s32[256]{0:T(256)} %reshape.31.sample_ref, s32[256]{0:T(256)} %reshape.32.count_ref, f32[8192]{0:T(1024)} %weight_ref.1, f32[4096,128]{1,0:T(8,128)} %get-tuple-element.8.wb_ref, bf16[4096,128]{1,0:T(8,128)(2,1)} %bitcast.7, bf16[256,128]{1,0:T(8,128)(2,1)} %get-tuple-element.9.values_ref), custom_call_target="tpu_custom_call" | custom-call | tf_op jit(solution)/shard_map/sketch/pallas_call | solution.py:301
  51.5 16.9 %all_to_all.15.in_ref = bf16[16,64,128]{2,1,0:T(8,128)(2,1)} all-to-all(bf16[16,64,128]{2,1,0:T(8,128)(2,1)} %sketch.1), channel_id=1, replica_groups=mesh['groups'=2,'row'=16] {'row'}, dimensions={0} | all-to-all | bytes 524288 | tf_op jit(solution)/shard_map/all_to_all | solution.py:312
  68.4 7.8 %solve.1 = (f32[64,512]{1,0:T(8,128)}, f32[16,8,128]{2,1,0:T(8,128)}) custom-call(bf16[16,64,128]{2,1,0:T(8,128)(2,1)} %all_to_all.15.in_ref), custom_call_target="tpu_custom_call" | custom-call | tf_op jit(solution)/shard_map/solve/pallas_call | solution.py:314
  76.2 11.0 %all_to_all.16.sums_ref = f32[16,8,128]{2,1,0:T(8,128)} all-to-all(f32[16,8,128]{2,1,0:T(8,128)} %get-tuple-element.10), channel_id=1, replica_groups=mesh['groups'=2,'row'=16] {'row'}, dimensions={0} | all-to-all | bytes 131072 | tf_op jit(solution)/shard_map/all_to_all | solution.py:327
  87.2 1.8 %scale.1 = (bf16[64,512]{1,0:T(8,128)(2,1)}, f32[1,64]{1,0:T(1,128)}) custom-call(f32[16,8,128]{2,1,0:T(8,128)} %all_to_all.16.sums_ref, f32[64,512]{1,0:T(8,128)} %get-tuple-element.11.update_ref), custom_call_target="tpu_custom_call" | custom-call | tf_op jit(solution)/shard_map/scale/pallas_call | solution.py:328
Async XLA Ops:
  0.6 19.7 %copy-start.2 = (s32[1,16,4,4]{1,3,2,0:T(4,128)S(1)}, s32[1,16,4,4]{1,3,2,0:T(4,128)}, u32[]{:S(2)}) copy-start(s32[1,16,4,4]{1,3,2,0:T(4,128)} %param.14) | copy-start | bytes 3076
  0.6 20.5 %copy-start.3 = (s32[1,16,4,4]{1,3,2,0:T(4,128)S(1)}, s32[1,16,4,4]{1,3,2,0:T(4,128)}, u32[]{:S(2)}) copy-start(s32[1,16,4,4]{1,3,2,0:T(4,128)} %param.15) | copy-start | bytes 3076
  0.7 21.2 %copy-start.1 = (f32[8192]{0:T(1024)S(1)}, f32[8192]{0:T(1024)}, u32[]{:S(2)}) copy-start(f32[8192]{0:T(1024)} %weight_ref.1) | copy-start | bytes 98308
  12.9 30.3 %all-to-all-start = ((bf16[16,256,128]{2,1,0:T(8,128)(2,1)}), bf16[16,256,128]{2,1,0:T(8,128)(2,1)S(1)}, u32[]{:S(2)}, u32[]{:S(2)}) async-start(bf16[16,256,128]{2,1,0:T(8,128)(2,1)} %bitcast.8), calls=%async_computation | async-start | bytes 2097152 | tf_op jit(solution)/shard_map/all_to_all | solution.py:279
  43.2 1.0 %copy-start = (bf16[16,256,128]{2,1,0:T(8,128)(2,1)}, bf16[16,256,128]{2,1,0:T(8,128)(2,1)S(1)}, u32[]{:S(2)}) copy-start(bf16[16,256,128]{2,1,0:T(8,128)(2,1)S(1)} %all-to-all-done) | copy-start | bytes 3145732

commit v5 on v4

--- a/solution.py
+++ b/solution.py
@@ -196,12 +196,18 @@
     sub = lax.broadcasted_iota(jnp.int32, (rank, LANES), 0)
     state = gram / total_samples + jnp.where(lane == sub, ridge, 0.0)
     lane_row = lane_index((1, LANES))
-    for k in range(rank):
-        pivot = 1.0 / state[k : k + 1, k : k + 1]
-        row = jnp.where(lane_row == k, 1.0, state[k : k + 1, :]) * pivot
-        column = state[:, k : k + 1]
-        rest = jnp.where(lane == k, 0.0, state)
-        state = jnp.where(sub == k, row, rest - column * row)
+    for k in range(0, rank, 2):
+        upper, lower = state[k : k + 1, :], state[k + 1 : k + 2, :]
+        p, q, r = upper[:, k : k + 1], upper[:, k + 1 : k + 2], lower[:, k + 1 : k + 2]
+        scale = 1.0 / (p * r - q * q)
+        here, after = lane_row == k, lane_row == k + 1
+        upper = jnp.where(here, 1.0, jnp.where(after, 0.0, upper))
+        lower = jnp.where(here, 0.0, jnp.where(after, 1.0, lower))
+        first = (r * upper - q * lower) * scale
+        last = (p * lower - q * upper) * scale
+        rest = jnp.where((lane == k) | (lane == k + 1), 0.0, state)
+        rest = rest - state[:, k : k + 1] * first - state[:, k + 1 : k + 2] * last
+        state = jnp.where(sub == k, first, jnp.where(sub == k + 1, last, rest))
     inverse = state[:, :rank]
     values = in_ref[:, :blocks, :].reshape(devices * blocks, LANES)
     rows = in_ref[:, blocks : 2 * blocks, :].reshape(devices * blocks, LANES).astype(f32)

time: 89.5 us -> 89.2 us (level)
  no operation moved by 1% of the time
where the time goes in v5:
time: 89.2 us; the launch traced here: 88.7 us
  Pallas kernels  42.8 us (48%)
  blocking collectives  28 us (31%)
  starting transfers between devices  7.43 us (8%)
  waiting for transfers between devices  6.75 us (8%)
  local copies, waits for them, and re-layouts  3.11 us (3%)
    all_to_all x1, blocking collectives, shards(): lax.all_to_all(payload, 'row', split_axis=0, concat_axis=0, tiled=True)  16.9 us
    pallas_call x1, Pallas kernels, shards(): pl.pallas_call(functools.partial(weighted_b_kernel, span=span), out_shape...  14 us
    pallas_call x1, Pallas kernels, shards(): pl.pallas_call(functools.partial(outgoing_kernel, span=span), out_shape=s...  12.3 us
    all_to_all x1, blocking collectives, shards(): lax.all_to_all(sums, 'row', split_axis=0, concat_axis=0, tiled=True)  11 us
    pallas_call x1, Pallas kernels, shards(): pl.pallas_call(functools.partial(solve_kernel, tiles=tiles, slots=slots,...  7.47 us
    all_to_all x1, starting transfers between devices, shards(): lax.all_to_all(c_out.reshape(devices, pairs // devices, LANES), 'row', sp...  7.43 us
    pallas_call x1, Pallas kernels, shards(): pl.pallas_call(functools.partial(sketch_kernel, span=span), out_shape=sha...  7.28 us
    all_to_all x1, waiting for transfers between devices, shards(): lax.all_to_all(c_out.reshape(devices, pairs // devices, LANES), 'row', sp...  6.75 us
  transfers between devices with their start and end apart: 1, of which 1 were waited for; matrix products, arithmetic and copies ran while one was open for 2% of the time, Pallas kernels for 16%

profile of v5, /device:TPU:0, one launch (start us, length us, event | category | flops | bytes accessed | tf_op | source)
XLA Modules:
  0.0 88.7 jit_solution(14592439637647745870)
XLA Ops:
  0.6 0.0 copy-start.2
  0.6 0.0 copy-start.3
  0.7 0.0 copy-start.1
  0.7 12.3 %outgoing.1 = bf16[4096,128]{1,0:T(8,128)(2,1)} custom-call(s32[1]{0:T(128)} %bitcast.base_ref, s32[64,128]{1,0:T(8,128)} %bitcast.10, bf16[64,4096]{1,0:T(8,128)(2,1)} %factor_ref.3), custom_call_target="tpu_custom_call" | custom-call | tf_op jit(solution)/shard_map/outgoing/pallas_call | solution.py:273
  12.9 7.4 %all-to-all-start = ((bf16[16,256,128]{2,1,0:T(8,128)(2,1)}), bf16[16,256,128]{2,1,0:T(8,128)(2,1)S(1)}, u32[]{:S(2)}, u32[]{:S(2)}) async-start(bf16[16,256,128]{2,1,0:T(8,128)(2,1)} %bitcast.8), calls=%async_computation | async-start | bytes 2097152 | tf_op jit(solution)/shard_map/all_to_all | solution.py:285
  20.4 0.0 copy-done.2
  20.4 0.1 copy.10
  20.5 0.6 reshape.31.sample_ref
  21.1 0.0 copy-done.3
  21.1 0.1 copy.11
  21.2 0.6 reshape.32.count_ref
  21.9 0.0 copy-done.1
  21.9 0.6 reshape.34.weight_ref
  22.5 14.0 %weighted_b.1 = (f32[4096,128]{1,0:T(8,128)}, bf16[256,128]{1,0:T(8,128)(2,1)}) custom-call(s32[1]{0:T(128)} %bitcast.base_ref, s32[256]{0:T(256)} %reshape.32.count_ref, s32[64,128]{1,0:T(8,128)} %bitcast.11, f32[32,256]{1,0:T(8,128)} %reshape.34.weight_ref, bf16[64,4096]{1,0:T(8,128)(2,1)} %factor_ref.2, bf16[256,128]{1,0:T(8,128)(2,1)} %bitcast.9), custom_call_target="tpu_custom_call" | custom-call | tf_op jit(solution)/shard_map/weighted_b/pallas_call | solution.py:288
  36.5 6.7 %all-to-all-done = bf16[16,256,128]{2,1,0:T(8,128)(2,1)S(1)} async-done(((bf16[16,256,128]{2,1,0:T(8,128)(2,1)}), bf16[16,256,128]{2,1,0:T(8,128)(2,1)S(1)}, u32[]{:S(2)}, u32[]{:S(2)}) %all-to-all-start) | async-done | bytes 1048608 | tf_op jit(solution)/shard_map/all_to_all | solution.py:285
  43.2 0.0 copy-start
  43.3 1.0 %copy-done = bf16[16,256,128]{2,1,0:T(8,128)(2,1)} copy-done((bf16[16,256,128]{2,1,0:T(8,128)(2,1)}, bf16[16,256,128]{2,1,0:T(8,128)(2,1)S(1)}, u32[]{:S(2)}) %copy-start) | copy-done | bytes 1048600
  44.2 7.3 %sketch.1 = bf16[16,64,128]{2,1,0:T(8,128)(2,1)} custom-call(s32[256]{0:T(256)} %reshape.31.sample_ref, s32[256]{0:T(256)} %reshape.32.count_ref, f32[8192]{0:T(1024)} %weight_ref.1, f32[4096,128]{1,0:T(8,128)} %get-tuple-element.8.wb_ref, bf16[4096,128]{1,0:T(8,128)(2,1)} %bitcast.7, bf16[256,128]{1,0:T(8,128)(2,1)} %get-tuple-element.9.values_ref), custom_call_target="tpu_custom_call" | custom-call | tf_op jit(solution)/shard_map/sketch/pallas_call | solution.py:307
  51.5 16.9 %all_to_all.15.in_ref = bf16[16,64,128]{2,1,0:T(8,128)(2,1)} all-to-all(bf16[16,64,128]{2,1,0:T(8,128)(2,1)} %sketch.1), channel_id=1, replica_groups=mesh['groups'=2,'row'=16] {'row'}, dimensions={0} | all-to-all | bytes 524288 | tf_op jit(solution)/shard_map/all_to_all | solution.py:318
  68.4 7.5 %solve.1 = (f32[64,512]{1,0:T(8,128)}, f32[16,8,128]{2,1,0:T(8,128)}) custom-call(bf16[16,64,128]{2,1,0:T(8,128)(2,1)} %all_to_all.15.in_ref), custom_call_target="tpu_custom_call" | custom-call | tf_op jit(solution)/shard_map/solve/pallas_call | solution.py:320
  75.9 11.0 %all_to_all.16.sums_ref = f32[16,8,128]{2,1,0:T(8,128)} all-to-all(f32[16,8,128]{2,1,0:T(8,128)} %get-tuple-element.10), channel_id=1, replica_groups=mesh['groups'=2,'row'=16] {'row'}, dimensions={0} | all-to-all | bytes 131072 | tf_op jit(solution)/shard_map/all_to_all | solution.py:333
  86.9 1.8 %scale.1 = (bf16[64,512]{1,0:T(8,128)(2,1)}, f32[1,64]{1,0:T(1,128)}) custom-call(f32[16,8,128]{2,1,0:T(8,128)} %all_to_all.16.sums_ref, f32[64,512]{1,0:T(8,128)} %get-tuple-element.11.update_ref), custom_call_target="tpu_custom_call" | custom-call | tf_op jit(solution)/shard_map/scale/pallas_call | solution.py:334
Async XLA Ops:
  0.6 19.7 %copy-start.2 = (s32[1,16,4,4]{1,3,2,0:T(4,128)S(1)}, s32[1,16,4,4]{1,3,2,0:T(4,128)}, u32[]{:S(2)}) copy-start(s32[1,16,4,4]{1,3,2,0:T(4,128)} %param.14) | copy-start | bytes 3076
  0.6 20.5 %copy-start.3 = (s32[1,16,4,4]{1,3,2,0:T(4,128)S(1)}, s32[1,16,4,4]{1,3,2,0:T(4,128)}, u32[]{:S(2)}) copy-start(s32[1,16,4,4]{1,3,2,0:T(4,128)} %param.15) | copy-start | bytes 3076
  0.7 21.2 %copy-start.1 = (f32[8192]{0:T(1024)S(1)}, f32[8192]{0:T(1024)}, u32[]{:S(2)}) copy-start(f32[8192]{0:T(1024)} %weight_ref.1) | copy-start | bytes 98308
  12.9 30.3 %all-to-all-start = ((bf16[16,256,128]{2,1,0:T(8,128)(2,1)}), bf16[16,256,128]{2,1,0:T(8,128)(2,1)S(1)}, u32[]{:S(2)}, u32[]{:S(2)}) async-start(bf16[16,256,128]{2,1,0:T(8,128)(2,1)} %bitcast.8), calls=%async_computation | async-start | bytes 2097152 | tf_op jit(solution)/shard_map/all_to_all | solution.py:285
  43.2 1.0 %copy-start = (bf16[16,256,128]{2,1,0:T(8,128)(2,1)}, bf16[16,256,128]{2,1,0:T(8,128)(2,1)S(1)}, u32[]{:S(2)}) copy-start(bf16[16,256,128]{2,1,0:T(8,128)(2,1)S(1)} %all-to-all-done) | copy-start | bytes 3145732
